TPU v7x, 128 devices: a whole 4x4x4 slice. The times are simulated.
128 devices in a mesh: rep: 2 (over core), fsdp: 64 (over z, y, x).
Axes of the slice: x: 4, y: 4, z: 4, core: 2. Of those that a mesh axis runs over, the one named last changes fastest.
Arguments:
- x_tokens: bfloat16 [768, 197, 1024], P(('rep', 'fsdp'))
- grad_z: bfloat16 [768, 197, 1024], P(('rep', 'fsdp'))
- w_qkv: float32 [1024, 3072], P('fsdp')
- b_qkv: float32 [3072], P('fsdp')
- w_out: float32 [1024, 1024], P('fsdp')
- w_up: float32 [1024, 4096], P('fsdp')
- b_up: float32 [4096], P('fsdp')
- w_down: float32 [4096, 1024], P('fsdp')
- vec_params: float32 [8, 1024], P(None, 'fsdp')
Outputs:
- output 1: bfloat16 [768, 197, 1024], P(('rep', 'fsdp'))
- output 2: bfloat16 [768, 197, 1024], P(('rep', 'fsdp'))
- output 3: float32 [1024, 3072], P('fsdp')
- output 4: float32 [3072], P('fsdp')
- output 5: float32 [1024, 1024], P('fsdp')
- output 6: float32 [1024, 4096], P('fsdp')
- output 7: float32 [4096], P('fsdp')
- output 8: float32 [4096, 1024], P('fsdp')
- output 9: float32 [8, 1024], P(None, 'fsdp')
All inputs are finite; a program needn't handle non-finite values.
Results may differ from a plain program's by a relative error of at most 0.02.
Values are sent between devices in bfloat16 or wider.
A program may use at most 1 GiB of HBM per device.

v0:
```python
import jax
import jax.numpy as jnp
from jax import lax
from jax.experimental import pallas as pl
from jax.experimental.pallas import tpu as pltpu
from jax.sharding import PartitionSpec as P

LN_EPS = 1e-5

ALL = ...
FIRST, ONE = 0, 1
PACK, SHARDS, FLAT, LANES, SPAN, TRIPLE, TILE = 16, 64, 192, 128, 256, 384, 512
SUBS, RING = 8, 4
CUBE, BLOCK = (RING,) * 3, (2, SUBS, LANES)
AXES, SIDES = range(3), range(2)
ONCE = pl.Buffered(ONE)
ANYWHERE = pl.BlockSpec(memory_space=pl.ANY)
VM = pltpu.VMEM
KEEP = True
MIN = float("-inf")


def row(ref, k):
    return ref[k:k + ONE, :]


def other(rep):
    return ONE - rep


def iota(dims, axis):
    return lax.broadcasted_iota(jnp.int32, dims, axis)


def loop(count, body, start, **options):
    return lax.fori_loop(FIRST, count, body, start, **options)


def sum_rows(t):
    return jnp.sum(t, axis=FIRST, keepdims=KEEP)


def max_rows(t):
    return jnp.max(t, axis=FIRST, keepdims=KEEP)


def sum_lanes(t):
    return jnp.sum(t, axis=-ONE, keepdims=KEEP)


def max_lanes(t):
    return jnp.max(t, axis=-ONE, keepdims=KEEP)


def mean_lanes(t):
    return jnp.mean(t, axis=-ONE, keepdims=KEEP)


SEQS, TOKENS, PAD, WIDTH, HIDDEN = 6, 197, 208, 1024, 4096
ROWS = SEQS * PAD
BF, F32 = jnp.bfloat16, jnp.float32
VMEM_CAP = 67043328


def nn(a, b):
    return lax.dot_general(a, b, (((1,), (0,)), ((), ())), preferred_element_type=F32)


def nt(a, b):
    return lax.dot_general(a, b, (((1,), (1,)), ((), ())), preferred_element_type=F32)


def tn(a, b):
    return lax.dot_general(a, b, (((0,), (0,)), ((), ())), preferred_element_type=F32)


def row_stats(t):
    mean = mean_lanes(t)
    centered = t - mean
    variance = mean_lanes(centered * centered)
    return centered, lax.rsqrt(variance + LN_EPS)


def norm_back(dt, xhat, rstd):
    return rstd * (dt - mean_lanes(dt) - xhat * mean_lanes(dt * xhat))


def head_halves(width=LANES):
    lane = iota((1, width), 1)
    return lane < SHARDS


def stack_heads(dst, rows, low):
    zero = jnp.zeros_like(rows)
    dst[:PAD] = jnp.where(low, rows, zero)
    dst[SPAN:SPAN + PAD] = jnp.where(low, zero, rows)


def padded(dst, base, rows_ref, s):
    dst[base + FLAT:base + PAD] = jnp.zeros((PACK, WIDTH), dst.dtype)
    dst[base:base + TOKENS] = rows_ref[s].astype(dst.dtype)


MESH_ID = pl.DeviceIdType.MESH
ORDERS = ((2, 1, 0), (1, 0, 2), (0, 2, 1))
HOPS = (1, 2, 3)
GREETED = 10
FAR, NEAR, DIRECT = "far", "near", "direct"
EVERY = slice(None)


def my_place():
    rep, flat = lax.axis_index("rep"), lax.axis_index("fsdp")
    return rep, (flat // PACK, (flat // RING) % RING, flat % RING)


def along(place, dim, shift):
    moved = list(place)
    moved[dim] = (place[dim] + shift) % RING
    return tuple(moved)


def flat_of(place):
    return place[0] * PACK + place[1] * 4 + place[2]


def greet(sem, rep, place):
    pl.semaphore_signal(sem, inc=1, device_id=(other(rep), flat_of(place)), device_id_type=MESH_ID)
    for dim in AXES:
        for shift in HOPS:
            pl.semaphore_signal(sem, inc=1, device_id=(rep, flat_of(along(place, dim, shift))), device_id_type=MESH_ID)


def entry_barrier(rep, place):
    barrier = pltpu.get_barrier_semaphore()
    greet(barrier, rep, place)
    pl.semaphore_wait(barrier, GREETED)


def ring_scratch(slots, stages, parts):
    dma = pltpu.SemaphoreType.DMA
    block = BLOCK
    cube, square, line = CUBE, CUBE[1:], CUBE[2:]
    sides = (parts, 3)
    buffers = [(slots, parts) + cube + block, (parts,) + cube + block, (parts,) + cube + block,
               (stages, parts) + square + block,
               (slots,) + sides + square + block, (stages,) + sides + line + block, (stages,) + sides + block]
    sems = [()] * 2 + [(slots, 2)] * 2 + [(stages, 2)] * 2 + [(stages,)] * 3
    regular = pltpu.SemaphoreType.REGULAR
    return [VM(b, F32) for b in buffers] + [dma(s) for s in sems] + [regular((slots,)), regular]


class Ring:
    def __init__(self, refs, slots, steps, window):
        (self.acc, self.inbox, self.outbox, self.rest, land0, land1, land2, self.pair_send, self.pair_recv,
         self.send, self.recv, self.rest_send, self.rest_recv, self.out_sem, self.out_send, self.out_recv,
         self.free, self.emptied) = refs
        self.landing = (land0, land1, land2)
        self.slots, self.steps, self.last = slots, steps, len(steps)
        self.window = window
        self.rep, self.place = my_place()
        self.partner = (other(self.rep), flat_of(self.place))

    def across(self, ref, send, recv, into=None):
        return pltpu.make_async_remote_copy(
            src_ref=ref, dst_ref=ref if into is None else into, send_sem=send, recv_sem=recv, device_id=self.partner,
            device_id_type=MESH_ID)

    def pair(self, parts):
        some = pl.ds(FIRST, parts)
        return self.across(self.outbox.at[some], self.pair_send, self.pair_recv, self.inbox.at[some])

    def sems(self, stage, step):
        phase, kind = step
        if phase:
            at = (stage, phase - 1)
            return self.rest_send.at[at], self.rest_recv.at[at]
        at = (stage % self.slots, 1 if kind == NEAR else 0)
        return self.send.at[at], self.recv.at[at]

    def landed(self, stage, parts, step):
        phase, kind = step
        at = self.home(stage, 0, phase)[1][:1] + (pl.ds(FIRST, parts),)
        sides = {FAR: 2, NEAR: pl.ds(FIRST, 2), DIRECT: EVERY}[kind]
        return self.across(self.landing[phase].at[at + (sides,)], *self.sems(stage, step))

    def axis(self, order, phase, index):
        at = {dim: EVERY for dim in order}
        for dim in order[:phase]:
            at[dim] = self.place[dim]
        at[order[phase]] = index
        if phase:
            del at[order[0]]
        return tuple(at[dim] for dim in sorted(at))

    def home(self, stage, part, phase):
        if phase:
            return self.rest, (stage, part)
        return self.acc, (stage % self.slots, part)

    def hops(self, stage, part, order, step):
        phase, kind = step
        dim = order[phase]
        memory, at = self.home(stage, part, phase)
        send, recv = self.sems(stage, step)
        found = []
        for side, shift in enumerate((1, 3) if kind != DIRECT else HOPS):
            source, target, place = shift, 0, at + (side,)
            if kind == FAR:
                source, target = 2, shift
            src = at + self.axis(order, phase, (self.place[dim] + source) % RING)
            into = at + self.axis(order, phase, (self.place[dim] + target) % RING)
            if kind == FAR:
                src, into, place = src + (side,), into + (side,), at + (2,) + (EVERY, EVERY, side)
            copy = pltpu.make_async_remote_copy(
                src_ref=memory.at[src], dst_ref=self.landing[phase].at[place], send_sem=send, recv_sem=recv,
                device_id=(self.rep, flat_of(along(self.place, dim, shift))), device_id_type=MESH_ID)
            found.append((copy, into, place))
        return found

    def results(self, stage, orders):
        for part, order in orders.items():
            src = self.rest.at[(stage, part) + tuple(self.place[dim] for dim in sorted(order[1:]))]
            dst = self.window(stage, part)
            pltpu.make_async_copy(src, dst, self.out_sem.at[stage]).start()
            self.across(src, self.out_send.at[stage], self.out_recv.at[stage], dst).start()

    def level(self, stage, level, orders, credit, refill):
        if level == 0:
            self.pair(len(orders)).wait()
            for part in orders:
                at = (stage % self.slots, part)
                for z in range(4):
                    self.acc[at + (z,)] = self.acc[at + (z,)] + self.inbox[part, z]

            @pl.when(stage >= self.slots)
            def _():
                pl.semaphore_wait(self.free.at[stage % self.slots], GREETED)

            @pl.when(refill)
            def _():
                pl.semaphore_signal(self.emptied, inc=1, device_id=self.partner, device_id_type=MESH_ID)
        else:
            step = self.steps[level - 1]
            phase, kind = step
            self.landed(stage, len(orders), step).wait_recv()
            for part, order in orders.items():
                memory = self.home(stage, part, phase)[0]
                hops = self.hops(stage, part, order, step)
                if kind == FAR:
                    for _, into, place in hops:
                        memory[into] = memory[into] + self.landing[phase][place]
                    continue
                into = hops[0][1]
                total = memory[into]
                for _, _, place in hops:
                    total = total + self.landing[phase][place]
                if phase:
                    memory[into] = total
                else:
                    self.rest[stage, part] = total
            if phase == 0 and kind != FAR:
                self.sent(stage, orders, (0,))

                @pl.when(credit)
                def _():
                    greet(self.free.at[stage % self.slots], self.rep, self.place)
        if level < self.last:
            for part, order in orders.items():
                for copy, _, _ in self.hops(stage, part, order, self.steps[level]):
                    copy.start()
        else:
            self.results(stage, orders)
            self.sent(stage, orders, (1, 2))

    def sent(self, stage, orders, phases):
        for step in self.steps:
            if step[0] in phases:
                self.landed(stage, len(orders), step).wait_send()

    def settle(self, stage, parts):
        ref = self.rest.at[stage, pl.ds(FIRST, parts), 0, 0]
        pltpu.make_async_copy(ref, ref, self.out_sem.at[stage]).wait()
        self.across(ref, self.out_send.at[stage], self.out_recv.at[stage]).wait()

    def reopen_box(self):
        pl.semaphore_wait(self.emptied, 1)


PIECE = TILE
QKV, OUT, UP, DOWN, SMALL = range(5)


def gather_items():
    rest = [(OUT, 0, 0, PIECE)]
    rest += [(UP, 0, PIECE * j, HIDDEN // 2) for j in range(4)]
    rest += [(DOWN, PACK * j, 0, PIECE) for j in range(4)]
    items = [(0, QKV, 0, PIECE * j, 3 * PIECE, ORDERS[j]) for j in AXES] + [(0, SMALL, 0, 0, 0, ORDERS[0])]
    return items + [(1 + k // 3,) + piece + (ORDERS[k % 3],) for k, piece in enumerate(rest)]


def small_rows(table, vec, b_qkv, b_up):
    lane = iota((SUBS, LANES), 1)

    def moved(f, half, shift):
        return pltpu.roll(table[f // PACK, f // RING % RING, f % RING, half], shift % LANES, 1)

    def fill(ref, tile, owners, half, width, first):
        total = jnp.zeros((SUBS, LANES), F32)
        for f in owners:
            start = width * f - LANES * tile
            here = jnp.logical_and(lane >= start, lane < start + width)
            total = jnp.where(here, moved(f, half, start - first), total)
        ref[:, tile * LANES:tile * LANES + LANES] = total[:ref.shape[0]]

    for tile in range(WIDTH // LANES):
        fill(vec, tile, range(SUBS * tile, SUBS * tile + SUBS), 0, PACK, 0)
    for tile in range(TILE // LANES):
        fill(b_up, tile, range(PACK * tile, PACK * tile + PACK), 1, SUBS, 0)
    for tile in range(3 * WIDTH // LANES):
        fill(b_qkv, tile, range(LANES * tile // 48, (LANES * tile + LANES - 1) // 48 + 1), 0, 48, PACK)


def placed(values, first, period=LANES):
    size = values.shape[ONE]
    lane = iota((size, LANES), 1)
    row = iota((size, LANES), 0)
    return nn(values.astype(BF), jnp.where(lane == row % period + first, 1.0, 0.0).astype(BF))


def unit_columns(j):
    column = iota((WIDTH, LANES), 1)
    row = iota((WIDTH, LANES), 0)
    taken = row == SHARDS * (column // SUBS) + SUBS * j + column % SUBS
    return jnp.where(taken, 1.0, 0.0).astype(BF)


def first_kernel(x_ref, dz_ref, sq_ref, so_ref, su_ref, sd_ref, bq_ref, bu_ref, sv_ref,
                 h1_ref, qkv_ref, o_ref, a_ref, h2_ref, dm_ref, vec_ref, bup_ref, wq_hbm, wo_hbm, wu_hbm, wd_hbm,
                 wq, wo, su, sd, packed, table, bias, xhat, kst, vst, xp,
                 own_sem, send_sem, recv_sem, pair_send, pair_recv, save_sem):
    t = pl.program_id(0)
    rep, place = my_place()
    partner = (other(rep), flat_of(place))
    items = gather_items()
    fulls = (wq, wo, wu_hbm, wd_hbm, table)

    def block(item, shards, half=None):
        _, array, row, first, step, _ = items[item]
        if array == SMALL:
            return table.at[shards + ((half,) if half is not None else ())]
        col, cols = rep * step + first, PIECE
        if half is not None:
            col, cols = col + half * (PIECE // 2), PIECE // 2
        return fulls[array].at[shards + (pl.ds(row, PACK), pl.ds(pl.multiple_of(col, LANES), cols))]

    def shard(item):
        _, array, row, first, step, _ = items[item]
        return (su, sd)[array - UP].at[pl.ds(row, PACK), pl.ds(pl.multiple_of(rep * step + first, LANES), PIECE)]

    def own(item):
        return pltpu.make_async_copy(shard(item), block(item, place), own_sem.at[item])

    def pair(item):
        everywhere = block(item, (EVERY,) * 3)
        return pltpu.make_async_remote_copy(
            src_ref=everywhere, dst_ref=everywhere, send_sem=pair_send.at[item], recv_sem=pair_recv.at[item],
            device_id=partner, device_id_type=MESH_ID)

    def hops(item, level):
        array, order = items[item][ONE], items[item][-1]
        phase, second = level // 2, level % 2
        dim = order[phase]
        found = []
        for side, shift in enumerate((1, 3)):
            at = [EVERY] * 3
            for later in order[phase:]:
                at[later] = place[later]
            if second:
                at[dim] = (place[dim] + 4 - shift) % RING
            dst = block(item, tuple(at), side if second else None)
            src = shard(item) if level == 0 and array in (UP, DOWN) else dst
            found.append(pltpu.make_async_remote_copy(
                src_ref=src, dst_ref=dst, send_sem=send_sem.at[item, level], recv_sem=recv_sem.at[item, level],
                device_id=(rep, flat_of(along(place, dim, shift))), device_id_type=MESH_ID))
        return found

    def both(item, level):
        order = items[item][-1]
        phase, second = level // 2, level % 2
        at = [EVERY] * 3
        for later in order[phase:]:
            at[later] = place[later]
        if not second:
            at[order[phase]] = pl.ds(FIRST, 2)
        ref = block(item, tuple(at))
        return pltpu.make_async_remote_copy(
            src_ref=ref, dst_ref=ref, send_sem=send_sem.at[item, level], recv_sem=recv_sem.at[item, level],
            device_id=partner, device_id_type=MESH_ID)

    def advance(*todo):
        for stage, level in todo:
            for item in range(len(items)):
                if items[item][FIRST] != stage:
                    continue
                if level:
                    both(item, level - 1).wait_recv()
                if level == 2 and items[item][ONE] in (UP, DOWN):
                    own(item).wait()
                if level == 6:
                    if items[item][ONE] != SMALL:
                        pair(item).start()
                else:
                    for copy in hops(item, level):
                        copy.start()

    def arrived(*arrays):
        for item in range(len(items)):
            if items[item][ONE] in arrays:
                pair(item).wait_recv()

    def saves():
        return (pltpu.make_async_copy(wq, wq_hbm, save_sem.at[FIRST]), pltpu.make_async_copy(wo, wo_hbm, save_sem.at[1]))

    @pl.when(t == FIRST)
    def _():
        for full, piece, half in ((wq, sq_ref, 3 * PIECE), (wo, so_ref, PIECE)):
            cols = pl.ds(pl.multiple_of(rep * half, LANES), half)
            full[place + (EVERY, cols)] = piece[:, cols].astype(BF)
        for b in range(4):
            packed[b * 16:b * PACK + PACK] = su_ref[:, b * WIDTH:b * WIDTH + WIDTH].astype(BF)
        sd[ALL] = sd_ref[ALL].astype(BF)
        first_row = iota((SUBS, 48), 0) == 0
        table[place + (0,)] = placed(sv_ref[ALL], 0) + placed(jnp.where(first_row, bq_ref[ALL], 0.0), PACK)
        unit = iota((SUBS, SHARDS), 1) // SUBS == iota((SUBS, SHARDS), 0)
        table[place + (1,)] = placed(jnp.where(unit, bu_ref[ALL], 0.0), 0, SUBS)
        entry_barrier(rep, place)
        advance((0, 0))
        for j in range(SUBS):
            turned = nn(packed[ALL], unit_columns(j)).astype(BF)
            for b in range(4):
                su[:, j * TILE + b * LANES:j * TILE + b * LANES + LANES] = turned[b * 16:b * PACK + PACK]
        for item in range(len(items)):
            if items[item][ONE] in (UP, DOWN):
                own(item).start()
        for s in range(SEQS):
            base = s * PAD
            xp[FLAT:PAD] = jnp.zeros((PACK, WIDTH), BF)
            xp[:TOKENS] = x_ref[s]
            centered, rstd = row_stats(xp[ALL].astype(F32))
            xhat[base:base + PAD] = centered * rstd
            level = s + 1
            if s < 5:
                advance(*((stage, level - stage) for stage in range(min(level, 3) + 1)))
        advance((0, 6))
        small_rows(table, vec_ref, bias, bup_ref)
        real = iota((PAD, 1), 0) < TOKENS

        def scaled(s, carry):
            here = pl.ds(pl.multiple_of(s * PAD, PACK), PAD)
            h1_ref[here, :] = jnp.where(real, xhat[here, :] * vec_ref[:1, :] + row(vec_ref, 1), 0.0).astype(BF)
            return carry

        loop(SEQS, scaled, 0)
        kst[ALL] = jnp.zeros_like(kst)
        vst[ALL] = jnp.zeros_like(vst)

    @pl.when(t > FIRST)
    def _():
        base = pl.multiple_of((t - 1) * (2 * PAD), PACK)

        def qkv_tile(n, carry):
            cols = pl.ds(pl.multiple_of((rep * 3 + n) % 6 * PIECE, PIECE), PIECE)
            weights = wq[:, :, :, :, cols].reshape(WIDTH, PIECE)
            qkv_ref[:, cols] = (nn(h1_ref[pl.ds(base, 2 * PAD), :], weights) + bias[:, cols]).astype(BF)
            return carry

        loop(3, qkv_tile, 0)

        @pl.when(t == 1)
        def _():
            arrived(QKV)
            saves()[0].start()

        lax.fori_loop(3, 6, qkv_tile, 0)

    @pl.when(t == 1)
    def _():
        advance((1, 5), (2, 4), (3, 3))

    low = head_halves()
    visible = iota((1, SPAN), 1) < TOKENS

    def head_pair(p, carry):
        def cols(third):
            return pl.ds(pl.multiple_of(third * WIDTH + p * LANES, LANES), LANES)

        for s in SIDES:
            rows = pl.ds(s * PAD, PAD)
            stack_heads(kst.at[s], qkv_ref[rows, cols(1)], low)
            stack_heads(vst.at[s], qkv_ref[rows, cols(2)], low)
        for s in SIDES:
            rows = pl.ds(s * PAD, PAD)
            scores = nt(qkv_ref[rows, cols(0)], kst[s])
            probs = []
            for half in SIDES:
                part = jnp.where(visible, scores[:, half * SPAN:half * SPAN + SPAN], -jnp.inf)
                top = max_lanes(part)
                e = jnp.exp((part - top) * 0.125)
                probs.append((e * (1.0 / sum_lanes(e))).astype(BF))
            o_ref[rows, pl.ds(pl.multiple_of(p * LANES, LANES), LANES)] = nn(jnp.concatenate(probs, axis=1), vst[s]).astype(BF)
        return carry

    def two_pairs(i, carry):
        head_pair(2 * i, carry)
        head_pair(2 * i + 1, carry)
        for step, turn, todo in ((1, 0, ((1, 6),)), (2, 1, ((3, 5),)), (1, 2, ((2, 5), (3, 4))), (2, 3, ((3, 6),))):
            @pl.when(jnp.logical_and(t == step, i == turn))
            def _(todo=todo):
                advance(*todo)

        return carry

    @pl.when(t > FIRST)
    def _():
        loop(4, two_pairs, 0)

    @pl.when(t == 1)
    def _():
        arrived(OUT)
        saves()[1].start()

    @pl.when(t > FIRST)
    def _():
        for s in SIDES:
            padded(xp, 0, x_ref, 2 * (t - 1) + s)
            xhat[s * PAD:s * PAD + PAD] = xp[ALL].astype(F32)
            dm_ref[s * PAD + FLAT:s * PAD + PAD] = jnp.zeros((PACK, WIDTH), BF)
            dm_ref[s * PAD:s * PAD + TOKENS] = (dz_ref[s].astype(F32) * row(vec_ref, 7)).astype(BF)
        a_ref[ALL] = nn(o_ref[ALL], wo[ALL].reshape(WIDTH, WIDTH)) + row(vec_ref, 2)

        def rows(i, carry):
            at = pl.ds(pl.multiple_of(i * 32, 32), 32)
            y = xhat[at, :] + row(vec_ref, 3) * a_ref[at, :]
            centered, rstd = row_stats(y)
            h2_ref[at, :] = (centered * rstd * row(vec_ref, 4) + row(vec_ref, 5)).astype(BF)
            return carry

        loop(2 * PAD // 32, rows, 0, unroll=13)

    @pl.when(t == 1)
    def _():
        advance((2, 6))

    @pl.when(t == 3)
    def _():
        arrived(UP, DOWN)
        for item in range(len(items)):
            if items[item][ONE] != SMALL:
                pair(item).wait_send()
            for level in range(6):
                both(item, level).wait_send()
        for copy in saves():
            copy.wait()


def first(x, dz, shards, small):
    whole = lambda dims: pl.BlockSpec(dims, lambda t: (0,) * len(dims), pipeline_mode=ONCE)
    pair = lambda t: jnp.maximum(t - 1, 0)
    rows = lambda width: pl.BlockSpec((2 * PAD, width), lambda t: (pair(t), 0))
    anywhere = ANYWHERE
    shape, vmem, dma = jax.ShapeDtypeStruct, VM, pltpu.SemaphoreType.DMA
    n = len(gather_items())
    cube = CUBE
    return pl.pallas_call(
        first_kernel, grid=(4,),
        out_shape=[shape((ROWS, WIDTH), BF), shape((ROWS, 3 * WIDTH), BF), shape((ROWS, WIDTH), BF), shape((ROWS, WIDTH), F32),
                   shape((ROWS, WIDTH), BF), shape((ROWS, WIDTH), BF), shape((SUBS, WIDTH), F32), shape((SUBS, TILE), F32)]
        + [shape(cube + s.shape, BF) for s in shards],
        in_specs=[whole((SEQS, TOKENS, WIDTH)), pl.BlockSpec((2, TOKENS, WIDTH), lambda t: (pair(t), 0, 0))]
        + [whole(s.shape) for s in shards + small],
        out_specs=[whole((ROWS, WIDTH)), rows(3 * WIDTH), rows(WIDTH), rows(WIDTH), rows(WIDTH), rows(WIDTH),
                   whole((SUBS, WIDTH)), whole((SUBS, TILE))] + [anywhere] * 4,
        scratch_shapes=[vmem(cube + shards[QKV].shape, BF), vmem(cube + shards[OUT].shape, BF), vmem(shards[UP].shape, BF),
                        vmem(shards[DOWN].shape, BF), vmem((SHARDS, WIDTH), BF), vmem(cube + (2, SUBS, LANES), F32), vmem((1, 3 * WIDTH), F32),
                        vmem((ROWS, WIDTH), F32), vmem((2, PIECE, LANES), BF), vmem((2, PIECE, LANES), BF),
                        vmem((PAD, WIDTH), BF),
                        dma((n,)), dma((n, 6)), dma((n, 6)), dma((n,)), dma((n,)), dma((2,))],
        compiler_params=pltpu.CompilerParams(vmem_limit_bytes=VMEM_CAP, collective_id=FIRST, has_side_effects=True),
        name="first",
    )(x, dz, *shards, *small)


CHUNK = 624
TILES = HIDDEN // TILE
MLP_SLOTS, MLP_PARTS = 3, 4
MLP_STEPS = ((0, FAR), (0, NEAR), (1, DIRECT), (2, DIRECT))


def gelu_and_slope(u):
    cdf = 0.5 * (1.0 + lax.erf(u * (2.0 ** -0.5)))
    pdf = jnp.exp(u * u * -0.5) * ((2.0 * jnp.pi) ** -0.5)
    return u * cdf, cdf + u * pdf


def mlp_kernel(h_ref, dm_ref, w1_ref, w2_ref, b1_ref, x_ref, dz_ref, a_ref, wo_ref, vec_ref,
               gw1_ref, gw2_ref, gb_ref, z_ref, gr_ref, da_ref, do_ref, gv_ref,
               m_acc, dh_acc, act, dpre, turned, xp, zp, zo, *ring_refs):
    j = pl.program_id(0)

    def window(stage, part):
        if part < 2:
            return gw2_ref.at[stage, pl.ds(rep * 4 + part * 2, 2)]
        return gw1_ref.at[:, stage * 4 + rep * 2 + part - 2]

    ring = Ring(ring_refs, MLP_SLOTS, MLP_STEPS, window)
    rep = ring.rep
    every_part = range(MLP_PARTS)

    def run(lag, level):
        stage = j - lag
        for turn in AXES:
            orders = {part: ORDERS[(turn + part) % 3] for part in every_part}

            @pl.when(jnp.logical_and(jnp.logical_and(stage >= 0, stage < TILES), stage % 3 == turn))
            def _(orders=orders):
                ring.level(stage, level, orders, stage < TILES - MLP_SLOTS, stage < TILES - 1)

    @pl.when(j == FIRST)
    def _():
        entry_barrier(rep, ring.place)
        m_acc[ALL] = jnp.zeros_like(m_acc)
        dh_acc[ALL] = jnp.zeros_like(dh_acc)
        turned[ALL] = jnp.transpose(h_ref[ALL])

    def chunk(i, total):
        at = pl.ds(pl.multiple_of(i * CHUNK, PACK), CHUNK)
        w1, w2 = w1_ref[ALL], w2_ref[ALL].reshape(TILE, WIDTH)
        u = nn(h_ref[at, :], w1) + b1_ref[pl.ds(j, 1), :]
        value, slope = gelu_and_slope(u)
        act[at, :] = value.astype(BF)
        d = nt(dm_ref[at, :], w2) * slope
        dpre[at, :] = d.astype(BF)
        m_acc[at, :] += nn(act[at, :], w2)
        dh_acc[at, :] += nt(dpre[at, :], w1)
        return sum_rows(d) + total

    def grads(core, target):
        cols = pl.ds(pl.multiple_of(core * TILE, TILE), TILE)
        g = tn(act[ALL], dm_ref[:, cols])
        for part in SIDES:
            for half in SIDES:
                first = (part * 2 + half) * LANES
                target(part, half, g[:, first:first + LANES].reshape(CUBE + BLOCK[1:]))

    def grads_up(core, target):
        g = nn(turned[ALL], dpre[:, pl.ds(pl.multiple_of(core * SPAN, SPAN), SPAN)])
        for part in SIDES:
            target(part + 2, EVERY, g[:, part * LANES:part * LANES + LANES].reshape(CUBE + BLOCK))

    @pl.when(j < TILES)
    def _():
        gb_ref[pl.ds(j, 1), :] = loop(ROWS // CHUNK, chunk, jnp.zeros((1, TILE), F32))

    @pl.when(j == TILES)
    def _():
        gv_ref[ALL] = jnp.zeros_like(gv_ref)

    @pl.when(j >= TILES)
    def _():
        padded(xp, 0, x_ref, 0)
        padded(zp, 0, dz_ref, 0)
        s1, g2, b2, s2 = (vec_ref[k:k + 1, :] for k in (3, 4, 6, 7))
        here = pl.ds(pl.multiple_of((j - TILES) * PAD, PACK), PAD)
        a = a_ref[ALL]
        y = xp[ALL].astype(F32) + s1 * a
        mlp_out = m_acc[here, :] + b2
        g_out = zp[ALL].astype(F32)
        zo[ALL] = (y + s2 * mlp_out).astype(BF)
        centered, rstd = row_stats(y)
        xhat = centered * rstd
        dh = dh_acc[here, :]
        g_resid = g_out + norm_back(dh * g2, xhat, rstd)
        d_att = g_resid * s1
        gr_ref[ALL] = g_resid
        da_ref[ALL] = d_att.astype(BF)
        for k, total in enumerate((d_att, g_resid * a, dh * xhat, dh, g_out * s2, g_out * mlp_out)):
            gv_ref[2 + k:3 + k, :] += sum_rows(total)
        z_ref[0] = zo[:TOKENS]
        do_ref[ALL] = nt(da_ref[ALL], wo_ref[ALL]).astype(BF)

    for lag in range(ring.last + 1, 0, -1):
        run(lag, lag - 1)

    @pl.when(j < TILES)
    def _():
        slot = j % MLP_SLOTS

        def out(part, half, value):
            ring.outbox[part, :, :, :, half] = value

        def own(part, half, value):
            ring.acc[slot, part, :, :, :, half] = value

        grads(other(rep), out)
        grads_up(other(rep), out)

        @pl.when(j >= 1)
        def _():
            ring.reopen_box()

        ring.pair(MLP_PARTS).start()
        grads(rep, own)
        grads_up(rep, own)

    @pl.when(j == TILES + SEQS - 1)
    def _():
        for stage in range(TILES):
            ring.settle(stage, MLP_PARTS)


def mlp(h, dm, w1, b1, w2, x, dz, a, w_out, vec):
    whole = lambda shape: pl.BlockSpec(shape, lambda j: (0, 0), pipeline_mode=ONCE)
    tile = lambda j: jnp.minimum(j, TILES - 1)
    seq = lambda j: jnp.maximum(j - TILES, 0)
    b1_spec = whole((SUBS, TILE))
    seqs = pl.BlockSpec((1, TOKENS, WIDTH), lambda j: (seq(j), 0, 0))
    rows = pl.BlockSpec((PAD, WIDTH), lambda j: (seq(j), 0))
    anywhere = ANYWHERE
    shape = jax.ShapeDtypeStruct
    return pl.pallas_call(
        mlp_kernel, grid=(TILES + SEQS,),
        out_shape=[shape((2, HIDDEN // LANES, SUBS, LANES), F32), shape((SUBS, SUBS, SUBS, LANES), F32), shape((SUBS, TILE), F32),
                   shape((SEQS, TOKENS, WIDTH), BF), shape((ROWS, WIDTH), F32), shape((ROWS, WIDTH), BF),
                   shape((ROWS, WIDTH), BF), shape((8, WIDTH), F32)],
        in_specs=[whole((ROWS, WIDTH)), whole((ROWS, WIDTH)), pl.BlockSpec((WIDTH, TILE), lambda j: (0, tile(j))),
                  pl.BlockSpec((SHARDS, SUBS, WIDTH), lambda j: (0, tile(j), 0)), b1_spec, seqs, seqs, rows,
                  whole((WIDTH, WIDTH)), whole((8, WIDTH))],
        out_specs=[anywhere, anywhere, whole((SUBS, TILE)), seqs, rows, rows, rows, whole((8, WIDTH))],
        scratch_shapes=[VM((ROWS, WIDTH), F32), VM((ROWS, WIDTH), F32), VM((ROWS, TILE), BF),
                        VM((ROWS, TILE), BF), VM((WIDTH, ROWS), BF), VM((PAD, WIDTH), BF),
                        VM((PAD, WIDTH), BF), VM((PAD, WIDTH), BF)] + ring_scratch(MLP_SLOTS, TILES, MLP_PARTS),
        compiler_params=pltpu.CompilerParams(vmem_limit_bytes=VMEM_CAP, collective_id=1, has_side_effects=True),
        name="mlp",
    )(h, dm, w1, w2.reshape(SHARDS, SHARDS, WIDTH), b1, x, dz, a, w_out, vec)


GROUP = SPAN
GROUPS = WIDTH // GROUP
THIRDS = 3
ATT_SLOTS, ATT_STAGES, ATT_PARTS = 2, GROUPS + 1, 4
ATT_STEPS = tuple((phase, DIRECT) for phase in AXES)


def small_blocks(target, vec, b_qkv, b_up):
    lane = iota((SUBS, LANES), 1)

    def turned(ref, tile, first, to):
        return pltpu.roll(ref[:, tile * LANES:tile * LANES + LANES], (to - first) % LANES, 1)

    for f in range(SHARDS):
        tile, first = divmod(48 * f, LANES)
        bias = turned(b_qkv, tile, first, PACK)
        if first + 48 > LANES:
            bias = jnp.where(lane[:1] < PACK + LANES - first, bias, turned(b_qkv, tile + 1, first, PACK))
        rows = turned(vec, f // SUBS, PACK * (f % SUBS), 0)
        up = turned(b_up, f // PACK, SUBS * (f % PACK), SHARDS)
        target[f // PACK, f // RING % RING, f % RING] = jnp.where(lane < PACK, rows, jnp.where(lane < SHARDS, bias, up))


def attn_bwd_kernel(q_ref, k_ref, v_ref, do_ref, h_ref, wq_ref, wk_ref, wv_ref, o_ref, da_ref, x_ref, gr_ref, vec_ref,
                    gvin_ref, gbup_ref, gup_ref, gw_ref, gwo_ref, dx_ref, small_ref, up_ref,
                    dh, grads, by_core, turned, qst, dst, xp, dxp, sums, biases, blocks, from_x, from_y, from_z, from_pair,
                    small_send, small_recv, *ring_refs):
    g = pl.program_id(0)

    def window(stage, part):
        if isinstance(stage, int) and stage == 0:
            return gwo_ref.at[:, rep * 4 + part]
        return gw_ref.at[:, part * SUBS + (stage - 1) * 2 + rep]

    ring = Ring(ring_refs, ATT_SLOTS, ATT_STEPS, window)
    rep, place = ring.rep, ring.place
    first_orders = {part: ORDERS[part % 3] for part in range(ATT_PARTS)}
    orders = {part: ORDERS[part] for part in range(THIRDS)}

    def level(stage, which, at):
        ring.level(stage, at, which, stage < ATT_STAGES - ATT_SLOTS, stage < ATT_STAGES - 1)

    def poll(todo):
        for lag, at in todo:
            @pl.when(g - lag >= 1)
            def _(lag=lag, at=at):
                level(g - lag, orders, at)

            @pl.when(g == lag)
            def _(at=at):
                level(0, first_orders, at)

    @pl.when(g == FIRST)
    def _():
        entry_barrier(rep, place)
        dh[ALL] = jnp.zeros_like(dh)
        qst[ALL] = jnp.zeros_like(qst)
        dst[ALL] = jnp.zeros_like(dst)
        turned[ALL] = jnp.transpose(h_ref[ALL])
        for core, box in ((other(rep), ring.outbox), (rep, ring.acc.at[FIRST])):
            w = tn(o_ref[ALL], da_ref[:, pl.ds(pl.multiple_of(core * TILE, TILE), TILE)])
            for part in range(ATT_PARTS):
                box[part] = w[:, part * LANES:part * LANES + LANES].reshape(CUBE + BLOCK)
            if box is ring.outbox:
                ring.pair(ATT_PARTS).start()

    poll(((2, 2),))
    low = head_halves()
    low_rows = iota((LANES, 1), 0) < SHARDS
    hidden = iota((PAD, 1), 0) >= TOKENS

    def seq(s, sums):
        rows = pl.ds(pl.multiple_of(s * PAD, PACK), PAD)
        out = []
        for p in SIDES:
            cols = slice(p * LANES, p * LANES + LANES)
            qs, ds = qst.at[p], dst.at[p]
            k_rows, v_rows = k_ref[rows, cols], v_ref[rows, cols]
            stack_heads(qs, q_ref[rows, cols], low)
            stack_heads(ds, do_ref[rows, cols], low)
            scores = jnp.where(hidden, -jnp.inf, nt(k_rows, qs[ALL]))
            top = max_rows(scores)
            e = jnp.exp((scores - top) * 0.125)
            probs = e * (1.0 / sum_rows(e))
            d_probs = nt(v_rows, ds[ALL])
            inner = sum_rows(d_probs * probs)
            d_scores = (probs * (d_probs - inner) * 0.125).astype(BF)
            grad_v = nn(probs.astype(BF), ds[ALL])
            grad_k = nn(d_scores, qs[ALL])
            folded = nn(jnp.transpose(k_rows), d_scores)
            grad_q = jnp.transpose(jnp.where(low_rows, folded[:, :SPAN], folded[:, SPAN:TILE]))[:PAD]
            for third, value in enumerate((grad_q, grad_k, grad_v)):
                rounded = value.astype(BF)
                grads[third, rows, cols] = rounded
                by_core[rows, p * TRIPLE + third * LANES:p * TRIPLE + third * LANES + LANES] = rounded
                out.append(sum_rows(value))
        return tuple(t + n for t, n in zip(sums, out))

    zero = jnp.zeros((ONE, LANES), F32)
    bias_sums = loop(SEQS, seq, (zero,) * 6, unroll=2)
    for p in SIDES:
        for third in range(THIRDS):
            at = pl.multiple_of(third * WIDTH + g * GROUP + p * LANES, LANES)
            biases[:, pl.ds(at, LANES)] = bias_sums[3 * p + third]
    poll(((2, 3), (1, 1), (0, 0)))
    stage = g + 1

    ring.reopen_box()

    w = nn(turned[ALL], by_core[ALL])
    for part in range(THIRDS):
        both = [w[:, at:at + LANES].reshape(CUBE + BLOCK) for at in (part * LANES, TRIPLE + part * LANES)]
        ring.outbox[part] = jnp.where(rep == 0, both[1], both[0])
        ring.acc[stage % ATT_SLOTS, part] = jnp.where(rep == 0, both[0], both[1])
    ring.pair(THIRDS).start()

    def chunk(i, carry):
        at = pl.ds(pl.multiple_of(i * CHUNK, PACK), CHUNK)
        dh[at, :] += nt(grads[0, at, :], wq_ref[ALL]) + nt(grads[1, at, :], wk_ref[ALL]) + nt(grads[2, at, :], wv_ref[ALL])
        return carry

    loop(ROWS // CHUNK, chunk, 0)

    def exchange(dim, landing, at, number):
        copies = []
        for hops in range(ONE, 4):
            index = list(at)
            index[dim] = (place[dim] + hops) % RING
            copies.append(pltpu.make_async_remote_copy(
                src_ref=blocks.at[tuple(index)], dst_ref=landing.at[hops - 1], send_sem=small_send.at[number + hops],
                recv_sem=small_recv.at[number + hops], device_id=(rep, flat_of(along(place, dim, hops))),
                device_id_type=MESH_ID))
        return copies

    def start(copies):
        for copy in copies:
            copy.start()
        return copies

    def collect(copies, dim, landing, at):
        for copy in copies:
            copy.wait()
        index = list(at)
        index[dim] = place[dim]
        index = tuple(index)
        blocks[index] = blocks[index] + landing[0] + landing[1] + landing[2]

    @pl.when(g == GROUPS - 1)
    def _():
        def tail(*todo):
            for stage, at in todo:
                level(stage, orders, at)

        gain = vec_ref[:1, :]
        tail((2, 2), (3, 1), (4, 0))
        sums[ALL] = gvin_ref[ALL]
        def norm_one(s, carry):
            padded(xp, 0, x_ref, s)
            here = pl.ds(pl.multiple_of(s * PAD, PACK), PAD)
            centered, rstd = row_stats(xp[ALL])
            xhat = centered * rstd
            d = dh[here, :]
            dxp[ALL] = (gr_ref[here, :] + norm_back(d * gain, xhat, rstd)).astype(BF)
            for k, value in enumerate((d * xhat, d)):
                sums[k:k + 1, :] += sum_rows(value)
            dx_ref[s] = dxp[:TOKENS]

            @pl.when(s == 3)
            def _():
                tail((2, 3), (3, 2))

            return carry

        loop(SEQS, norm_one, 0)
        small_blocks(blocks, sums, biases, gbup_ref)
        at = [EVERY] * 3
        number = 0
        def shard_order():
            for j in range(SUBS):
                turned[:, j * LANES:j * LANES + LANES] = unit_columns(j)
                for b in range(4):
                    for h in SIDES:
                        xp[b * PACK + h * SUBS:b * PACK + h * SUBS + SUBS, j * LANES:j * LANES + LANES] = gup_ref[h, j * 4 + b]
            left = xp[:SHARDS]
            total = jnp.zeros_like(left)
            for _ in AXES:
                piece = left.astype(BF)
                total = total + nt(piece, turned[:, :WIDTH])
                left = left - piece.astype(F32)
            for b in range(4):
                up_ref[:, b * WIDTH:b * WIDTH + WIDTH] = total[b * 16:b * PACK + PACK]

        for dim, landing, todo in ((2, from_x, ((4, 1),)), (1, from_y, ((3, 3),)), (0, from_z, ((4, 2),))):
            copies = start(exchange(dim, landing, at, number))
            if dim == 1:
                shard_order()
            tail(*todo)
            collect(copies, dim, landing, at)
            at[dim] = place[dim]
            number += 3
        last = pltpu.make_async_remote_copy(
            src_ref=blocks.at[place], dst_ref=from_pair, send_sem=small_send.at[FIRST], recv_sem=small_recv.at[FIRST],
            device_id=ring.partner, device_id_type=MESH_ID)
        last.start()
        tail((4, 3))
        last.wait()
        small_ref[ALL] = blocks[place] + from_pair[ALL]
        ring.settle(0, ATT_PARTS)
        for stage in range(ONE, ATT_STAGES):
            ring.settle(stage, THIRDS)


def attn_bwd(qkv, do, h, w_qkv, o, da, x, gr, vec, gvin, gbup, gup):
    one = lambda shape: pl.BlockSpec(shape, lambda g: (0,) * len(shape), pipeline_mode=ONCE)
    third = lambda t: pl.BlockSpec((ROWS, GROUP), lambda g: (0, t * GROUPS + g))
    wthird = lambda t: pl.BlockSpec((WIDTH, GROUP), lambda g: (0, t * GROUPS + g))
    col = pl.BlockSpec((ROWS, GROUP), lambda g: (0, g))
    anywhere = ANYWHERE
    shape = jax.ShapeDtypeStruct
    rows = (SUBS, LANES)
    vmem, dma = VM, pltpu.SemaphoreType.DMA
    return pl.pallas_call(
        attn_bwd_kernel, grid=(GROUPS,),
        out_shape=[shape((2, 3 * SUBS) + rows, F32), shape((2, SUBS) + rows, F32), shape((SEQS, TOKENS, WIDTH), BF), shape(rows, F32), shape((PACK, HIDDEN), F32)],
        in_specs=[third(0), third(1), third(2), col, one((ROWS, WIDTH)), wthird(0), wthird(1), wthird(2),
                  one((ROWS, WIDTH)), one((ROWS, WIDTH)), one((SEQS, TOKENS, WIDTH)), one((ROWS, WIDTH)),
                  one((SUBS, WIDTH)), one((SUBS, WIDTH)), one((SUBS, TILE)), one(gup.shape)],
        out_specs=[anywhere, anywhere, one((SEQS, TOKENS, WIDTH)), one(rows), one((PACK, HIDDEN))],
        scratch_shapes=[vmem((ROWS, WIDTH), F32), vmem((THIRDS, ROWS, GROUP), BF), vmem((ROWS, 3 * GROUP), BF),
                        vmem((WIDTH, ROWS), BF), vmem((2, TILE, LANES), BF), vmem((2, TILE, LANES), BF),
                        vmem((PAD, WIDTH), F32), vmem((PAD, WIDTH), BF), vmem((SUBS, WIDTH), F32), vmem((1, 3 * WIDTH), F32),
                        vmem(CUBE + rows, F32), vmem((3, 4, 4) + rows, F32), vmem((3, 4) + rows, F32),
                        vmem((3,) + rows, F32), vmem(rows, F32), dma((10,)), dma((10,))]
        + ring_scratch(ATT_SLOTS, ATT_STAGES, ATT_PARTS),
        compiler_params=pltpu.CompilerParams(vmem_limit_bytes=VMEM_CAP, collective_id=2, has_side_effects=True),
        name="attn_bwd",
    )(qkv, qkv, qkv, do, h, w_qkv, w_qkv, w_qkv, o, da, x, gr, vec, gvin, gbup, gup)


def layer(x, dz, w_qkv, b_qkv, w_out, w_up, b_up, w_down, vec_params):
    h1, qkv, o, a, h2, dm, vec, b_up, w_qkv, w_out, w_up, w_down = first(
        x, dz, (w_qkv, w_out, w_up, w_down), (b_qkv[None], b_up[None], vec_params))
    w_qkv, w_out, w_up = (w.reshape(WIDTH, -1) for w in (w_qkv, w_out, w_up))
    gw_up, gw_down, gb_up, z, gr, da, do, gvec = mlp(h2, dm, w_up, b_up, w_down, x, dz, a, w_out, vec)
    gw_qkv, gw_out, dx, small, gw_up = attn_bwd(qkv, do, h1, w_qkv, o, da, x, gr, vec, gvec, gb_up, gw_up)
    plain = lambda g: g.swapaxes(1, 2).reshape(g.shape[0] * SUBS, -1)
    return (z, dx, plain(gw_qkv), small[0, 16:SHARDS], plain(gw_out), gw_up, small[:, 64:72].reshape(SHARDS),
            plain(gw_down), small[:, :PACK])


def solution(mesh):
    batch = P(("rep", "fsdp"), None, None)
    rows, flat = P("fsdp", None), P("fsdp")
    params = (rows, flat, rows, rows, flat, rows, P(None, "fsdp"))
    return jax.shard_map(layer, mesh=mesh, in_specs=(batch, batch) + params, out_specs=(batch, batch) + params, check_vma=False)
```

profile of v0, /device:TPU:1, one launch (start us, length us, event | category | flops | bytes accessed | tf_op | source)
XLA Modules:
  0.0 336.7 jit_solution(4725287135357775745)
XLA Ops:
  0.6 99.0 %first.1 = (bf16[1248,1024]{1,0:T(8,128)(2,1)}, bf16[1248,3072]{1,0:T(8,128)(2,1)}, bf16[1248,1024]{1,0:T(8,128)(2,1)}, f32[1248,1024]{1,0:T(8,128)}, bf16[1248,...) custom-call(bf16[6,197,1024]{2,1,0:T(8,128)(2,1)} %x_ref.5, ...), custom_call_target="tpu_custom_call" | custom-call | tf_op jit(solution)/shard_map/first/pallas_call | solution.py:575
  99.6 131.3 %mlp.1 = (f32[2,32,8,128]{3,2,1,0:T(8,128)}, f32[8,8,8,128]{3,2,1,0:T(8,128)}, f32[8,512]{1,0:T(8,128)}, bf16[6,197,1024]{2,1,0:T(8,128)(2,1)}, f32[1248,1024]{1...) custom-call(bf16[1248,1024]{1,0:T(8,128)(2,1)} %get-tuple-element.34.h_ref, ...), custom_call_target="tpu_custom_call" | custom-call | tf_op jit(solution)/shard_map/mlp/pallas_call | solution.py:731
  230.9 94.8 %attn_bwd.1 = (f32[2,24,8,128]{3,2,1,0:T(8,128)}, f32[2,8,8,128]{3,2,1,0:T(8,128)}, bf16[6,197,1024]{2,1,0:T(8,128)(2,1)}, f32[8,128]{1,0:T(8,128)}, f32[16,4096]{1,0:T(8,128)}) custom-call(bf16[1248,3072]{1,0:T(8,128)(2,1)} %get-tuple-element.43.q_ref.k_ref.v_ref, bf16[1248,3072]{1,0:T(8,128)(2,1)} %get-tuple-element.43.q_ref.k_ref.v_ref, ...), custom_call_target="tpu_custom_call" | custom-call | tf_op jit(solution)/shard_map/attn_bwd/pallas_call | solution.py:969
  325.7 0.0 copy-start
  325.7 1.4 slice_bitcast_fusion
  327.2 0.7 slice.10
  327.9 0.6 reshape.48
  328.5 3.4 %copy.25 = bf16[6,197,1024]{2,1,0:T(8,128)(2,1)} copy(bf16[6,197,1024]{2,1,0:T(8,128)(2,1)} %get-tuple-element.68) | data formatting | bytes 4841472
  331.9 0.0 copy-done
  331.9 0.0 copy-start.3
  331.9 0.0 copy-start.4
  331.9 0.0 copy-start.1
  331.9 0.0 copy-start.5
  331.9 1.4 copy.26
  333.4 0.0 copy-done.3
  333.4 0.7 copy.27
  334.1 0.0 copy-done.4
  334.1 0.6 copy.28
  334.7 0.0 copy-done.2
  334.7 0.7 copy.29
  335.4 0.0 copy-done.1
  335.4 0.7 copy.30
  336.1 0.0 copy-done.5
  336.1 0.6 copy.31
  (1 shorter events, 0.0 us)
Async XLA Ops:
  325.7 6.2 %copy-start = (bf16[6,197,1024]{2,1,0:T(8,128)(2,1)S(1)}, bf16[6,197,1024]{2,1,0:T(8,128)(2,1)}, u32[]{:S(2)}) copy-start(bf16[6,197,1024]{2,1,0:T(8,128)(2,1)} %get-tuple-element.69) | copy-start | bytes 7262212
  331.9 1.5 copy-start.3
  331.9 2.2 copy-start.4
  331.9 2.8 copy-start.2
  331.9 3.5 %copy-start.1 = (f32[8,8,8,128]{3,2,1,0:T(8,128)S(1)}, f32[8,8,8,128]{3,2,1,0:T(8,128)}, u32[]{:S(2)}) copy-start(f32[8,8,8,128]{3,2,1,0:T(8,128)} %get-tuple-element.58) | copy-start | bytes 786436
  331.9 4.2 %copy-start.5 = (f32[8,128]{1,0:T(8,128)S(1)}, f32[8,128]{1,0:T(8,128)}, u32[]{:S(2)}) copy-start(f32[8,128]{1,0:T(8,128)} %get-tuple-element.55) | copy-start | bytes 12292
where the time goes:
time: 337 us
  Pallas kernels  325 us (96%)
  local copies, waits for them, and re-layouts  10.9 us (3%)
    pallas_call x1, Pallas kernels, mlp(): pl.pallas_call(mlp_kernel, grid=(TILES + SEQS,), out_shape=[shape((2, HID...  131 us
    pallas_call x1, Pallas kernels, first(): pl.pallas_call(first_kernel, grid=(4,), out_shape=[shape((ROWS, WIDTH), B...  99 us
    pallas_call x1, Pallas kernels, attn_bwd(): pl.pallas_call(attn_bwd_kernel, grid=(GROUPS,), out_shape=[shape((2, 3 *...  94.8 us
    unnamed x19, local copies, waits for them, and re-layouts  8.18 us

commit v1 on v0

--- a/solution.py
+++ b/solution.py
@@ -17,7 +17,8 @@
 ANYWHERE = pl.BlockSpec(memory_space=pl.ANY)
 VM = pltpu.VMEM
 KEEP = True
-MIN = float("-inf")
+UNIT, NIL = 1.0, 0.0
+TILE_SHAPE = BLOCK[ONE:]
 
 
 def row(ref, k):
@@ -287,23 +288,26 @@
         pl.semaphore_wait(self.emptied, 1)
 
 
+THIRDS = 3
 PIECE = TILE
 QKV, OUT, UP, DOWN, SMALL = range(5)
 
 
 def gather_items():
+    items = [(half, QKV, 0, third * WIDTH + half * PIECE, PIECE // 2, PIECE // 2, ORDERS[third])
+             for half in SIDES for third in range(THIRDS)]
     rest = [(OUT, 0, 0, PIECE)]
     rest += [(UP, 0, PIECE * j, HIDDEN // 2) for j in range(4)]
     rest += [(DOWN, PACK * j, 0, PIECE) for j in range(4)]
-    items = [(0, QKV, 0, PIECE * j, 3 * PIECE, ORDERS[j]) for j in AXES] + [(0, SMALL, 0, 0, 0, ORDERS[0])]
-    return items + [(1 + k // 3,) + piece + (ORDERS[k % 3],) for k, piece in enumerate(rest)]
+    items += [(2 + k // 3,) + piece + (PIECE, ORDERS[k % 3]) for k, piece in enumerate(rest)]
+    return items + [(0, SMALL, 0, 0, 0, 0, ORDERS[0])]
 
 
 def small_rows(table, vec, b_qkv, b_up):
-    lane = iota((SUBS, LANES), 1)
+    lane = iota((SUBS, LANES), ONE)
 
     def moved(f, half, shift):
-        return pltpu.roll(table[f // PACK, f // RING % RING, f % RING, half], shift % LANES, 1)
+        return pltpu.roll(table[f // PACK, f // RING % RING, f % RING, half], shift % LANES, ONE)
 
     def fill(ref, tile, owners, half, width, first):
         total = jnp.zeros((SUBS, LANES), F32)
@@ -323,16 +327,16 @@
 
 def placed(values, first, period=LANES):
     size = values.shape[ONE]
-    lane = iota((size, LANES), 1)
-    row = iota((size, LANES), 0)
-    return nn(values.astype(BF), jnp.where(lane == row % period + first, 1.0, 0.0).astype(BF))
+    lane = iota((size, LANES), ONE)
+    row = iota((size, LANES), FIRST)
+    return nn(values.astype(BF), jnp.where(lane == row % period + first, UNIT, NIL).astype(BF))
 
 
 def unit_columns(j):
-    column = iota((WIDTH, LANES), 1)
-    row = iota((WIDTH, LANES), 0)
+    column = iota((WIDTH, LANES), ONE)
+    row = iota((WIDTH, LANES), FIRST)
     taken = row == SHARDS * (column // SUBS) + SUBS * j + column % SUBS
-    return jnp.where(taken, 1.0, 0.0).astype(BF)
+    return jnp.where(taken, UNIT, NIL).astype(BF)
 
 
 def first_kernel(x_ref, dz_ref, sq_ref, so_ref, su_ref, sd_ref, bq_ref, bu_ref, sv_ref,
@@ -346,16 +350,17 @@
     fulls = (wq, wo, wu_hbm, wd_hbm, table)
 
     def block(item, shards, half=None):
-        _, array, row, first, step, _ = items[item]
+        _, array, row, first, step, cols, _ = items[item]
         if array == SMALL:
             return table.at[shards + ((half,) if half is not None else ())]
-        col, cols = rep * step + first, PIECE
+        col = rep * step + first
         if half is not None:
-            col, cols = col + half * (PIECE // 2), PIECE // 2
+            cols = cols // 2
+            col = col + half * cols
         return fulls[array].at[shards + (pl.ds(row, PACK), pl.ds(pl.multiple_of(col, LANES), cols))]
 
     def shard(item):
-        _, array, row, first, step, _ = items[item]
+        _, array, row, first, step, _, _ = items[item]
         return (su, sd)[array - UP].at[pl.ds(row, PACK), pl.ds(pl.multiple_of(rep * step + first, LANES), PIECE)]
 
     def own(item):
@@ -414,9 +419,9 @@
                     for copy in hops(item, level):
                         copy.start()
 
-    def arrived(*arrays):
+    def arrived(*stages):
         for item in range(len(items)):
-            if items[item][ONE] in arrays:
+            if items[item][FIRST] in stages and items[item][ONE] != SMALL:
                 pair(item).wait_recv()
 
     def saves():
@@ -424,18 +429,19 @@
 
     @pl.when(t == FIRST)
     def _():
-        for full, piece, half in ((wq, sq_ref, 3 * PIECE), (wo, so_ref, PIECE)):
-            cols = pl.ds(pl.multiple_of(rep * half, LANES), half)
-            full[place + (EVERY, cols)] = piece[:, cols].astype(BF)
+        for _, array, _, first, step, width, _ in items:
+            if array in (QKV, OUT):
+                cols = pl.ds(pl.multiple_of(rep * step + first, LANES), width)
+                (wq, wo)[array][place + (EVERY, cols)] = (sq_ref, so_ref)[array][:, cols].astype(BF)
         for b in range(4):
             packed[b * 16:b * PACK + PACK] = su_ref[:, b * WIDTH:b * WIDTH + WIDTH].astype(BF)
         sd[ALL] = sd_ref[ALL].astype(BF)
         first_row = iota((SUBS, 48), 0) == 0
-        table[place + (0,)] = placed(sv_ref[ALL], 0) + placed(jnp.where(first_row, bq_ref[ALL], 0.0), PACK)
-        unit = iota((SUBS, SHARDS), 1) // SUBS == iota((SUBS, SHARDS), 0)
-        table[place + (1,)] = placed(jnp.where(unit, bu_ref[ALL], 0.0), 0, SUBS)
+        table[place + (0,)] = placed(sv_ref[ALL], 0) + placed(jnp.where(first_row, bq_ref[ALL], NIL), PACK)
+        unit = iota((SUBS, SHARDS), ONE) // SUBS == iota((SUBS, SHARDS), FIRST)
+        table[place + (1,)] = placed(jnp.where(unit, bu_ref[ALL], NIL), 0, SUBS)
         entry_barrier(rep, place)
-        advance((0, 0))
+        advance((0, 0), (1, 0))
         for j in range(SUBS):
             turned = nn(packed[ALL], unit_columns(j)).astype(BF)
             for b in range(4):
@@ -443,57 +449,62 @@
         for item in range(len(items)):
             if items[item][ONE] in (UP, DOWN):
                 own(item).start()
-        for s in range(SEQS):
+        later = (2, 3, 4)
+        advance(*((stage, 0) for stage in later))
+        everything = (0, 1) + later
+        for s, todo in enumerate((
+                [(stage, 1) for stage in everything], [(stage, 2) for stage in everything], [(0, 3), (1, 3)],
+                [(0, 4), (1, 4)] + [(stage, 3) for stage in later], [(0, 5), (2, 4)], [(0, 6), (1, 5)])):
             base = s * PAD
             xp[FLAT:PAD] = jnp.zeros((PACK, WIDTH), BF)
             xp[:TOKENS] = x_ref[s]
             centered, rstd = row_stats(xp[ALL].astype(F32))
             xhat[base:base + PAD] = centered * rstd
-            level = s + 1
-            if s < 5:
-                advance(*((stage, level - stage) for stage in range(min(level, 3) + 1)))
-        advance((0, 6))
+            advance(*todo)
         small_rows(table, vec_ref, bias, bup_ref)
         real = iota((PAD, 1), 0) < TOKENS
 
         def scaled(s, carry):
             here = pl.ds(pl.multiple_of(s * PAD, PACK), PAD)
-            h1_ref[here, :] = jnp.where(real, xhat[here, :] * vec_ref[:1, :] + row(vec_ref, 1), 0.0).astype(BF)
+            h1_ref[here, :] = jnp.where(real, xhat[here, :] * vec_ref[:1, :] + row(vec_ref, 1), NIL).astype(BF)
             return carry
 
         loop(SEQS, scaled, 0)
         kst[ALL] = jnp.zeros_like(kst)
         vst[ALL] = jnp.zeros_like(vst)
 
+    half, seqs = jnp.maximum(t - ONE, FIRST) // 3, jnp.maximum(t - ONE, FIRST) % 3
+    base = pl.multiple_of(seqs * (2 * PAD), PACK)
+
+    @pl.when(t == 1)
+    def _():
+        arrived(0)
+
+    @pl.when(t == 4)
+    def _():
+        arrived(1)
+        saves()[0].start()
+
     @pl.when(t > FIRST)
     def _():
-        base = pl.multiple_of((t - 1) * (2 * PAD), PACK)
-
-        def qkv_tile(n, carry):
-            cols = pl.ds(pl.multiple_of((rep * 3 + n) % 6 * PIECE, PIECE), PIECE)
+        for third in range(THIRDS):
+            cols = pl.ds(pl.multiple_of(third * WIDTH + half * PIECE, PIECE), PIECE)
             weights = wq[:, :, :, :, cols].reshape(WIDTH, PIECE)
-            qkv_ref[:, cols] = (nn(h1_ref[pl.ds(base, 2 * PAD), :], weights) + bias[:, cols]).astype(BF)
-            return carry
-
-        loop(3, qkv_tile, 0)
-
-        @pl.when(t == 1)
-        def _():
-            arrived(QKV)
-            saves()[0].start()
-
-        lax.fori_loop(3, 6, qkv_tile, 0)
+            qkv = nn(h1_ref[pl.ds(base, 2 * PAD), :], weights) + bias[:, cols]
+            qkv_ref[:, third * PIECE:third * PIECE + PIECE] = qkv.astype(BF)
 
     @pl.when(t == 1)
     def _():
-        advance((1, 5), (2, 4), (3, 3))
+        advance((3, 4))
 
     low = head_halves()
     visible = iota((1, SPAN), 1) < TOKENS
 
+    half_cols = half * PIECE
+
     def head_pair(p, carry):
         def cols(third):
-            return pl.ds(pl.multiple_of(third * WIDTH + p * LANES, LANES), LANES)
+            return pl.ds(pl.multiple_of(third * PIECE + p * LANES, LANES), LANES)
 
         for s in SIDES:
             rows = pl.ds(s * PAD, PAD)
@@ -503,41 +514,44 @@
             rows = pl.ds(s * PAD, PAD)
             scores = nt(qkv_ref[rows, cols(0)], kst[s])
             probs = []
-            for half in SIDES:
-                part = jnp.where(visible, scores[:, half * SPAN:half * SPAN + SPAN], -jnp.inf)
+            for head in SIDES:
+                part = jnp.where(visible, scores[:, head * SPAN:head * SPAN + SPAN], -jnp.inf)
                 top = max_lanes(part)
                 e = jnp.exp((part - top) * 0.125)
                 probs.append((e * (1.0 / sum_lanes(e))).astype(BF))
-            o_ref[rows, pl.ds(pl.multiple_of(p * LANES, LANES), LANES)] = nn(jnp.concatenate(probs, axis=1), vst[s]).astype(BF)
+            here = pl.ds(pl.multiple_of(base + s * PAD, PACK), PAD)
+            heads = pl.ds(pl.multiple_of(half_cols + p * LANES, LANES), LANES)
+            o_ref[here, heads] = nn(jnp.concatenate(probs, axis=1), vst[s]).astype(BF)
         return carry
 
     def two_pairs(i, carry):
         head_pair(2 * i, carry)
         head_pair(2 * i + 1, carry)
-        for step, turn, todo in ((1, 0, ((1, 6),)), (2, 1, ((3, 5),)), (1, 2, ((2, 5), (3, 4))), (2, 3, ((3, 6),))):
+        for step, turn, todo in ((1, 0, (1, 6)), (1, 1, (2, 5)), (2, 0, (4, 4)), (2, 1, (3, 5)), (3, 0, (2, 6)),
+                                 (4, 1, (4, 5)), (5, 0, (3, 6)), (5, 1, (4, 6))):
             @pl.when(jnp.logical_and(t == step, i == turn))
             def _(todo=todo):
-                advance(*todo)
+                advance(todo)
 
         return carry
 
     @pl.when(t > FIRST)
     def _():
-        loop(4, two_pairs, 0)
-
-    @pl.when(t == 1)
-    def _():
-        arrived(OUT)
+        loop(2, two_pairs, 0)
+
+    @pl.when(t == 4)
+    def _():
+        arrived(2)
         saves()[1].start()
 
-    @pl.when(t > FIRST)
+    @pl.when(t > 3)
     def _():
         for s in SIDES:
-            padded(xp, 0, x_ref, 2 * (t - 1) + s)
+            padded(xp, 0, x_ref, 2 * seqs + s)
             xhat[s * PAD:s * PAD + PAD] = xp[ALL].astype(F32)
             dm_ref[s * PAD + FLAT:s * PAD + PAD] = jnp.zeros((PACK, WIDTH), BF)
             dm_ref[s * PAD:s * PAD + TOKENS] = (dz_ref[s].astype(F32) * row(vec_ref, 7)).astype(BF)
-        a_ref[ALL] = nn(o_ref[ALL], wo[ALL].reshape(WIDTH, WIDTH)) + row(vec_ref, 2)
+        a_ref[ALL] = nn(o_ref[pl.ds(base, 2 * PAD), :], wo[ALL].reshape(WIDTH, WIDTH)) + row(vec_ref, 2)
 
         def rows(i, carry):
             at = pl.ds(pl.multiple_of(i * 32, 32), 32)
@@ -548,13 +562,9 @@
 
         loop(2 * PAD // 32, rows, 0, unroll=13)
 
-    @pl.when(t == 1)
-    def _():
-        advance((2, 6))
-
-    @pl.when(t == 3)
-    def _():
-        arrived(UP, DOWN)
+    @pl.when(t == 6)
+    def _():
+        arrived(3, 4)
         for item in range(len(items)):
             if items[item][ONE] != SMALL:
                 pair(item).wait_send()
@@ -566,20 +576,22 @@
 
 def first(x, dz, shards, small):
     whole = lambda dims: pl.BlockSpec(dims, lambda t: (0,) * len(dims), pipeline_mode=ONCE)
-    pair = lambda t: jnp.maximum(t - 1, 0)
-    rows = lambda width: pl.BlockSpec((2 * PAD, width), lambda t: (pair(t), 0))
+    pair = lambda t: jnp.maximum(t - RING, FIRST)
+    past = lambda t: jnp.maximum(t - ONE, FIRST)
+    rows = pl.BlockSpec((2 * PAD, WIDTH), lambda t: (pair(t), 0))
+    halves = pl.BlockSpec((2 * PAD, 3 * PIECE), lambda t: (past(t) % 3, past(t) // 3))
     anywhere = ANYWHERE
     shape, vmem, dma = jax.ShapeDtypeStruct, VM, pltpu.SemaphoreType.DMA
     n = len(gather_items())
     cube = CUBE
     return pl.pallas_call(
-        first_kernel, grid=(4,),
+        first_kernel, grid=(7,),
         out_shape=[shape((ROWS, WIDTH), BF), shape((ROWS, 3 * WIDTH), BF), shape((ROWS, WIDTH), BF), shape((ROWS, WIDTH), F32),
                    shape((ROWS, WIDTH), BF), shape((ROWS, WIDTH), BF), shape((SUBS, WIDTH), F32), shape((SUBS, TILE), F32)]
         + [shape(cube + s.shape, BF) for s in shards],
         in_specs=[whole((SEQS, TOKENS, WIDTH)), pl.BlockSpec((2, TOKENS, WIDTH), lambda t: (pair(t), 0, 0))]
         + [whole(s.shape) for s in shards + small],
-        out_specs=[whole((ROWS, WIDTH)), rows(3 * WIDTH), rows(WIDTH), rows(WIDTH), rows(WIDTH), rows(WIDTH),
+        out_specs=[whole((ROWS, WIDTH)), halves, whole((ROWS, WIDTH)), rows, rows, rows,
                    whole((SUBS, WIDTH)), whole((SUBS, TILE))] + [anywhere] * 4,
         scratch_shapes=[vmem(cube + shards[QKV].shape, BF), vmem(cube + shards[OUT].shape, BF), vmem(shards[UP].shape, BF),
                         vmem(shards[DOWN].shape, BF), vmem((SHARDS, WIDTH), BF), vmem(cube + (2, SUBS, LANES), F32), vmem((1, 3 * WIDTH), F32),
@@ -651,7 +663,7 @@
         for part in SIDES:
             for half in SIDES:
                 first = (part * 2 + half) * LANES
-                target(part, half, g[:, first:first + LANES].reshape(CUBE + BLOCK[1:]))
+                target(part, half, g[:, first:first + LANES].reshape(CUBE + TILE_SHAPE))
 
     def grads_up(core, target):
         g = nn(turned[ALL], dpre[:, pl.ds(pl.multiple_of(core * SPAN, SPAN), SPAN)])
@@ -722,7 +734,7 @@
 def mlp(h, dm, w1, b1, w2, x, dz, a, w_out, vec):
     whole = lambda shape: pl.BlockSpec(shape, lambda j: (0, 0), pipeline_mode=ONCE)
     tile = lambda j: jnp.minimum(j, TILES - 1)
-    seq = lambda j: jnp.maximum(j - TILES, 0)
+    seq = lambda j: jnp.maximum(j - TILES, FIRST)
     b1_spec = whole((SUBS, TILE))
     seqs = pl.BlockSpec((1, TOKENS, WIDTH), lambda j: (seq(j), 0, 0))
     rows = pl.BlockSpec((PAD, WIDTH), lambda j: (seq(j), 0))
@@ -747,16 +759,15 @@
 
 GROUP = SPAN
 GROUPS = WIDTH // GROUP
-THIRDS = 3
 ATT_SLOTS, ATT_STAGES, ATT_PARTS = 2, GROUPS + 1, 4
 ATT_STEPS = tuple((phase, DIRECT) for phase in AXES)
 
 
 def small_blocks(target, vec, b_qkv, b_up):
-    lane = iota((SUBS, LANES), 1)
+    lane = iota((SUBS, LANES), ONE)
 
     def turned(ref, tile, first, to):
-        return pltpu.roll(ref[:, tile * LANES:tile * LANES + LANES], (to - first) % LANES, 1)
+        return pltpu.roll(ref[:, tile * LANES:tile * LANES + LANES], (to - first) % LANES, ONE)
 
     for f in range(SHARDS):
         tile, first = divmod(48 * f, LANES)
@@ -813,7 +824,7 @@
 
     poll(((2, 2),))
     low = head_halves()
-    low_rows = iota((LANES, 1), 0) < SHARDS
+    low_rows = iota((LANES, ONE), 0) < SHARDS
     hidden = iota((PAD, 1), 0) >= TOKENS
 
     def seq(s, sums):
@@ -959,7 +970,7 @@
 
 def attn_bwd(qkv, do, h, w_qkv, o, da, x, gr, vec, gvin, gbup, gup):
     one = lambda shape: pl.BlockSpec(shape, lambda g: (0,) * len(shape), pipeline_mode=ONCE)
-    third = lambda t: pl.BlockSpec((ROWS, GROUP), lambda g: (0, t * GROUPS + g))
+    third = lambda t: pl.BlockSpec((ROWS, GROUP), lambda g: (0, g // 2 * 6 + t * 2 + g % 2))
     wthird = lambda t: pl.BlockSpec((WIDTH, GROUP), lambda g: (0, t * GROUPS + g))
     col = pl.BlockSpec((ROWS, GROUP), lambda g: (0, g))
     anywhere = ANYWHERE

time: 337 us -> 326 us (0.967)
  Pallas kernels: 325 us -> 315 us
    pallas_call x1, Pallas kernels: 99 us -> 87.6 us  [first(): pl.pallas_call(first_kernel, grid=(7,), out_shape=[shape((ROWS, WIDTH), B...]
where the time goes in v1:
time: 326 us
  Pallas kernels  315 us (97%)
  local copies, waits for them, and re-layouts  10.9 us (3%)
    pallas_call x1, Pallas kernels, mlp(): pl.pallas_call(mlp_kernel, grid=(TILES + SEQS,), out_shape=[shape((2, HID...  132 us
    pallas_call x1, Pallas kernels, attn_bwd(): pl.pallas_call(attn_bwd_kernel, grid=(GROUPS,), out_shape=[shape((2, 3 *...  95.5 us
    pallas_call x1, Pallas kernels, first(): pl.pallas_call(first_kernel, grid=(7,), out_shape=[shape((ROWS, WIDTH), B...  87.6 us
    unnamed x19, local copies, waits for them, and re-layouts  8.18 us

profile of v1, /device:TPU:1, one launch (start us, length us, event | category | flops | bytes accessed | tf_op | source)
XLA Modules:
  0.0 326.2 jit_solution(204989305860746523)
XLA Ops:
  0.6 87.6 %first.1 = (bf16[1248,1024]{1,0:T(8,128)(2,1)}, bf16[1248,3072]{1,0:T(8,128)(2,1)}, bf16[1248,1024]{1,0:T(8,128)(2,1)}, f32[1248,1024]{1,0:T(8,128)}, bf16[1248,...) custom-call(bf16[6,197,1024]{2,1,0:T(8,128)(2,1)} %x_ref.5, ...), custom_call_target="tpu_custom_call" | custom-call | tf_op jit(solution)/shard_map/first/pallas_call | solution.py:587
  88.3 131.5 %mlp.1 = (f32[2,32,8,128]{3,2,1,0:T(8,128)}, f32[8,8,8,128]{3,2,1,0:T(8,128)}, f32[8,512]{1,0:T(8,128)}, bf16[6,197,1024]{2,1,0:T(8,128)(2,1)}, f32[1248,1024]{1...) custom-call(bf16[1248,1024]{1,0:T(8,128)(2,1)} %get-tuple-element.34.h_ref, ...), custom_call_target="tpu_custom_call" | custom-call | tf_op jit(solution)/shard_map/mlp/pallas_call | solution.py:743
  219.8 95.5 %attn_bwd.1 = (f32[2,24,8,128]{3,2,1,0:T(8,128)}, f32[2,8,8,128]{3,2,1,0:T(8,128)}, bf16[6,197,1024]{2,1,0:T(8,128)(2,1)}, f32[8,128]{1,0:T(8,128)}, f32[16,4096]{1,0:T(8,128)}) custom-call(bf16[1248,3072]{1,0:T(8,128)(2,1)} %get-tuple-element.43.q_ref.k_ref.v_ref, bf16[1248,3072]{1,0:T(8,128)(2,1)} %get-tuple-element.43.q_ref.k_ref.v_ref, ...), custom_call_target="tpu_custom_call" | custom-call | tf_op jit(solution)/shard_map/attn_bwd/pallas_call | solution.py:980
  315.3 0.0 copy-start
  315.3 1.4 slice_bitcast_fusion
  316.7 0.7 slice.10
  317.4 0.6 reshape.48
  318.0 3.4 %copy.25 = bf16[6,197,1024]{2,1,0:T(8,128)(2,1)} copy(bf16[6,197,1024]{2,1,0:T(8,128)(2,1)} %get-tuple-element.68) | data formatting | bytes 4841472
  321.4 0.0 copy-done
  321.4 0.0 copy-start.3
  321.4 0.0 copy-start.4
  321.4 0.0 copy-start.1
  321.5 0.0 copy-start.5
  321.5 1.4 copy.26
  322.9 0.0 copy-done.3
  322.9 0.7 copy.27
  323.6 0.0 copy-done.4
  323.6 0.6 copy.28
  324.2 0.0 copy-done.2
  324.2 0.7 copy.29
  324.9 0.0 copy-done.1
  324.9 0.7 copy.30
  325.6 0.0 copy-done.5
  325.6 0.6 copy.31
  (1 shorter events, 0.0 us)
Async XLA Ops:
  315.3 6.2 %copy-start = (bf16[6,197,1024]{2,1,0:T(8,128)(2,1)S(1)}, bf16[6,197,1024]{2,1,0:T(8,128)(2,1)}, u32[]{:S(2)}) copy-start(bf16[6,197,1024]{2,1,0:T(8,128)(2,1)} %get-tuple-element.69) | copy-start | bytes 7262212
  321.4 1.5 copy-start.3
  321.4 2.2 copy-start.4
  321.4 2.8 copy-start.2
  321.4 3.5 %copy-start.1 = (f32[8,8,8,128]{3,2,1,0:T(8,128)S(1)}, f32[8,8,8,128]{3,2,1,0:T(8,128)}, u32[]{:S(2)}) copy-start(f32[8,8,8,128]{3,2,1,0:T(8,128)} %get-tuple-element.58) | copy-start | bytes 786436
  321.5 4.2 %copy-start.5 = (f32[8,128]{1,0:T(8,128)S(1)}, f32[8,128]{1,0:T(8,128)}, u32[]{:S(2)}) copy-start(f32[8,128]{1,0:T(8,128)} %get-tuple-element.55) | copy-start | bytes 12292

commit v2 on v1

--- a/solution.py
+++ b/solution.py
@@ -8,7 +8,7 @@
 LN_EPS = 1e-5
 
 ALL = ...
-FIRST, ONE = 0, 1
+FIRST, ONE, PAIR, THREE = range(4)
 PACK, SHARDS, FLAT, LANES, SPAN, TRIPLE, TILE = 16, 64, 192, 128, 256, 384, 512
 SUBS, RING = 8, 4
 CUBE, BLOCK = (RING,) * 3, (2, SUBS, LANES)
@@ -122,7 +122,7 @@
 
 
 def flat_of(place):
-    return place[0] * PACK + place[1] * 4 + place[2]
+    return place[0] * PACK + place[1] * RING + place[2]
 
 
 def greet(sem, rep, place):
@@ -146,7 +146,7 @@
     buffers = [(slots, parts) + cube + block, (parts,) + cube + block, (parts,) + cube + block,
                (stages, parts) + square + block,
                (slots,) + sides + square + block, (stages,) + sides + line + block, (stages,) + sides + block]
-    sems = [()] * 2 + [(slots, 2)] * 2 + [(stages, 2)] * 2 + [(stages,)] * 3
+    sems = [()] * PAIR + [(slots, 2)] * PAIR + [(stages, 2)] * PAIR + [(stages,)] * THREE
     regular = pltpu.SemaphoreType.REGULAR
     return [VM(b, F32) for b in buffers] + [dma(s) for s in sems] + [regular((slots,)), regular]
 
@@ -294,12 +294,12 @@
 
 
 def gather_items():
-    items = [(half, QKV, 0, third * WIDTH + half * PIECE, PIECE // 2, PIECE // 2, ORDERS[third])
+    items = [(half, QKV, 0, third * WIDTH + half * PIECE, PIECE // PAIR, PIECE // PAIR, ORDERS[third])
              for half in SIDES for third in range(THIRDS)]
     rest = [(OUT, 0, 0, PIECE)]
-    rest += [(UP, 0, PIECE * j, HIDDEN // 2) for j in range(4)]
+    rest += [(UP, 0, PIECE * j, HIDDEN // PAIR) for j in range(4)]
     rest += [(DOWN, PACK * j, 0, PIECE) for j in range(4)]
-    items += [(2 + k // 3,) + piece + (PIECE, ORDERS[k % 3]) for k, piece in enumerate(rest)]
+    items += [(2 + k // THREE,) + piece + (PIECE, ORDERS[k % THREE]) for k, piece in enumerate(rest)]
     return items + [(0, SMALL, 0, 0, 0, 0, ORDERS[0])]
 
 
@@ -321,7 +321,7 @@
         fill(vec, tile, range(SUBS * tile, SUBS * tile + SUBS), 0, PACK, 0)
     for tile in range(TILE // LANES):
         fill(b_up, tile, range(PACK * tile, PACK * tile + PACK), 1, SUBS, 0)
-    for tile in range(3 * WIDTH // LANES):
+    for tile in range(THREE * WIDTH // LANES):
         fill(b_qkv, tile, range(LANES * tile // 48, (LANES * tile + LANES - 1) // 48 + 1), 0, 48, PACK)
 
 
@@ -340,9 +340,9 @@
 
 
 def first_kernel(x_ref, dz_ref, sq_ref, so_ref, su_ref, sd_ref, bq_ref, bu_ref, sv_ref,
-                 h1_ref, qkv_ref, o_ref, a_ref, h2_ref, dm_ref, vec_ref, bup_ref, wq_hbm, wo_hbm, wu_hbm, wd_hbm,
+                 h1_hbm, qkv_ref, o_hbm, a_ref, h2_ref, dm_ref, vec_ref, bup_ref, wq_hbm, wo_hbm, wu_hbm, wd_hbm,
                  wq, wo, su, sd, packed, table, bias, xhat, kst, vst, xp,
-                 own_sem, send_sem, recv_sem, pair_send, pair_recv, save_sem):
+                 own_sem, send_sem, recv_sem, pair_send, pair_recv, save_sem, h1_ref, o_ref, o_sem):
     t = pl.program_id(0)
     rep, place = my_place()
     partner = (other(rep), flat_of(place))
@@ -355,7 +355,7 @@
             return table.at[shards + ((half,) if half is not None else ())]
         col = rep * step + first
         if half is not None:
-            cols = cols // 2
+            cols = cols // PAIR
             col = col + half * cols
         return fulls[array].at[shards + (pl.ds(row, PACK), pl.ds(pl.multiple_of(col, LANES), cols))]
 
@@ -367,18 +367,18 @@
         return pltpu.make_async_copy(shard(item), block(item, place), own_sem.at[item])
 
     def pair(item):
-        everywhere = block(item, (EVERY,) * 3)
+        everywhere = block(item, (EVERY,) * THREE)
         return pltpu.make_async_remote_copy(
             src_ref=everywhere, dst_ref=everywhere, send_sem=pair_send.at[item], recv_sem=pair_recv.at[item],
             device_id=partner, device_id_type=MESH_ID)
 
     def hops(item, level):
         array, order = items[item][ONE], items[item][-1]
-        phase, second = level // 2, level % 2
+        phase, second = level // PAIR, level % PAIR
         dim = order[phase]
         found = []
         for side, shift in enumerate((1, 3)):
-            at = [EVERY] * 3
+            at = [EVERY] * THREE
             for later in order[phase:]:
                 at[later] = place[later]
             if second:
@@ -392,8 +392,8 @@
 
     def both(item, level):
         order = items[item][-1]
-        phase, second = level // 2, level % 2
-        at = [EVERY] * 3
+        phase, second = level // PAIR, level % PAIR
+        at = [EVERY] * THREE
         for later in order[phase:]:
             at[later] = place[later]
         if not second:
@@ -425,7 +425,12 @@
                 pair(item).wait_recv()
 
     def saves():
-        return (pltpu.make_async_copy(wq, wq_hbm, save_sem.at[FIRST]), pltpu.make_async_copy(wo, wo_hbm, save_sem.at[1]))
+        return (pltpu.make_async_copy(wq, wq_hbm, save_sem.at[FIRST]), pltpu.make_async_copy(wo, wo_hbm, save_sem.at[1]),
+                pltpu.make_async_copy(h1_ref, h1_hbm, save_sem.at[2]))
+
+    def heads_out(number):
+        rows = pl.ds(number * (PAIR * PAD), PAIR * PAD)
+        return pltpu.make_async_copy(o_ref.at[rows], o_hbm.at[rows], o_sem.at[number])
 
     @pl.when(t == FIRST)
     def _():
@@ -473,12 +478,13 @@
         kst[ALL] = jnp.zeros_like(kst)
         vst[ALL] = jnp.zeros_like(vst)
 
-    half, seqs = jnp.maximum(t - ONE, FIRST) // 3, jnp.maximum(t - ONE, FIRST) % 3
-    base = pl.multiple_of(seqs * (2 * PAD), PACK)
+    half, seqs = jnp.maximum(t - ONE, FIRST) // THREE, jnp.maximum(t - ONE, FIRST) % THREE
+    base = pl.multiple_of(seqs * (PAIR * PAD), PACK)
 
     @pl.when(t == 1)
     def _():
         arrived(0)
+        saves()[2].start()
 
     @pl.when(t == 4)
     def _():
@@ -490,7 +496,7 @@
         for third in range(THIRDS):
             cols = pl.ds(pl.multiple_of(third * WIDTH + half * PIECE, PIECE), PIECE)
             weights = wq[:, :, :, :, cols].reshape(WIDTH, PIECE)
-            qkv = nn(h1_ref[pl.ds(base, 2 * PAD), :], weights) + bias[:, cols]
+            qkv = nn(h1_ref[pl.ds(base, PAIR * PAD), :], weights) + bias[:, cols]
             qkv_ref[:, third * PIECE:third * PIECE + PIECE] = qkv.astype(BF)
 
     @pl.when(t == 1)
@@ -525,8 +531,8 @@
         return carry
 
     def two_pairs(i, carry):
-        head_pair(2 * i, carry)
-        head_pair(2 * i + 1, carry)
+        head_pair(PAIR * i, carry)
+        head_pair(PAIR * i + 1, carry)
         for step, turn, todo in ((1, 0, (1, 6)), (1, 1, (2, 5)), (2, 0, (4, 4)), (2, 1, (3, 5)), (3, 0, (2, 6)),
                                  (4, 1, (4, 5)), (5, 0, (3, 6)), (5, 1, (4, 6))):
             @pl.when(jnp.logical_and(t == step, i == turn))
@@ -539,6 +545,11 @@
     def _():
         loop(2, two_pairs, 0)
 
+    for number in AXES:
+        @pl.when(t == 4 + number)
+        def _(number=number):
+            heads_out(number).start()
+
     @pl.when(t == 4)
     def _():
         arrived(2)
@@ -547,11 +558,11 @@
     @pl.when(t > 3)
     def _():
         for s in SIDES:
-            padded(xp, 0, x_ref, 2 * seqs + s)
+            padded(xp, 0, x_ref, PAIR * seqs + s)
             xhat[s * PAD:s * PAD + PAD] = xp[ALL].astype(F32)
             dm_ref[s * PAD + FLAT:s * PAD + PAD] = jnp.zeros((PACK, WIDTH), BF)
             dm_ref[s * PAD:s * PAD + TOKENS] = (dz_ref[s].astype(F32) * row(vec_ref, 7)).astype(BF)
-        a_ref[ALL] = nn(o_ref[pl.ds(base, 2 * PAD), :], wo[ALL].reshape(WIDTH, WIDTH)) + row(vec_ref, 2)
+        a_ref[ALL] = nn(o_ref[pl.ds(base, PAIR * PAD), :], wo[ALL].reshape(WIDTH, WIDTH)) + row(vec_ref, 2)
 
         def rows(i, carry):
             at = pl.ds(pl.multiple_of(i * 32, 32), 32)
@@ -560,7 +571,7 @@
             h2_ref[at, :] = (centered * rstd * row(vec_ref, 4) + row(vec_ref, 5)).astype(BF)
             return carry
 
-        loop(2 * PAD // 32, rows, 0, unroll=13)
+        loop(PAIR * PAD // 32, rows, 0, unroll=13)
 
     @pl.when(t == 6)
     def _():
@@ -572,32 +583,34 @@
                 both(item, level).wait_send()
         for copy in saves():
             copy.wait()
+        for number in AXES:
+            heads_out(number).wait()
 
 
 def first(x, dz, shards, small):
     whole = lambda dims: pl.BlockSpec(dims, lambda t: (0,) * len(dims), pipeline_mode=ONCE)
     pair = lambda t: jnp.maximum(t - RING, FIRST)
     past = lambda t: jnp.maximum(t - ONE, FIRST)
-    rows = pl.BlockSpec((2 * PAD, WIDTH), lambda t: (pair(t), 0))
-    halves = pl.BlockSpec((2 * PAD, 3 * PIECE), lambda t: (past(t) % 3, past(t) // 3))
+    rows = pl.BlockSpec((PAIR * PAD, WIDTH), lambda t: (pair(t), 0))
+    halves = pl.BlockSpec((PAIR * PAD, THREE * PIECE), lambda t: (past(t) % THREE, past(t) // THREE))
     anywhere = ANYWHERE
     shape, vmem, dma = jax.ShapeDtypeStruct, VM, pltpu.SemaphoreType.DMA
     n = len(gather_items())
     cube = CUBE
     return pl.pallas_call(
         first_kernel, grid=(7,),
-        out_shape=[shape((ROWS, WIDTH), BF), shape((ROWS, 3 * WIDTH), BF), shape((ROWS, WIDTH), BF), shape((ROWS, WIDTH), F32),
+        out_shape=[shape((ROWS, WIDTH), BF), shape((ROWS, THREE * WIDTH), BF), shape((ROWS, WIDTH), BF), shape((ROWS, WIDTH), F32),
                    shape((ROWS, WIDTH), BF), shape((ROWS, WIDTH), BF), shape((SUBS, WIDTH), F32), shape((SUBS, TILE), F32)]
         + [shape(cube + s.shape, BF) for s in shards],
         in_specs=[whole((SEQS, TOKENS, WIDTH)), pl.BlockSpec((2, TOKENS, WIDTH), lambda t: (pair(t), 0, 0))]
         + [whole(s.shape) for s in shards + small],
-        out_specs=[whole((ROWS, WIDTH)), halves, whole((ROWS, WIDTH)), rows, rows, rows,
-                   whole((SUBS, WIDTH)), whole((SUBS, TILE))] + [anywhere] * 4,
+        out_specs=[anywhere, halves, anywhere, rows, rows, rows,
+                   whole((SUBS, WIDTH)), whole((SUBS, TILE))] + [anywhere] * RING,
         scratch_shapes=[vmem(cube + shards[QKV].shape, BF), vmem(cube + shards[OUT].shape, BF), vmem(shards[UP].shape, BF),
-                        vmem(shards[DOWN].shape, BF), vmem((SHARDS, WIDTH), BF), vmem(cube + (2, SUBS, LANES), F32), vmem((1, 3 * WIDTH), F32),
+                        vmem(shards[DOWN].shape, BF), vmem((SHARDS, WIDTH), BF), vmem(cube + (2, SUBS, LANES), F32), vmem((1, THREE * WIDTH), F32),
                         vmem((ROWS, WIDTH), F32), vmem((2, PIECE, LANES), BF), vmem((2, PIECE, LANES), BF),
                         vmem((PAD, WIDTH), BF),
-                        dma((n,)), dma((n, 6)), dma((n, 6)), dma((n,)), dma((n,)), dma((2,))],
+                        dma((n,)), dma((n, 6)), dma((n, 6)), dma((n,)), dma((n,)), dma((3,)), vmem((ROWS, WIDTH), BF), vmem((ROWS, WIDTH), BF), dma((3,))],
         compiler_params=pltpu.CompilerParams(vmem_limit_bytes=VMEM_CAP, collective_id=FIRST, has_side_effects=True),
         name="first",
     )(x, dz, *shards, *small)
@@ -622,8 +635,8 @@
 
     def window(stage, part):
         if part < 2:
-            return gw2_ref.at[stage, pl.ds(rep * 4 + part * 2, 2)]
-        return gw1_ref.at[:, stage * 4 + rep * 2 + part - 2]
+            return gw2_ref.at[stage, pl.ds(rep * RING + part * PAIR, 2)]
+        return gw1_ref.at[:, stage * RING + rep * PAIR + part - 2]
 
     ring = Ring(ring_refs, MLP_SLOTS, MLP_STEPS, window)
     rep = ring.rep
@@ -632,9 +645,9 @@
     def run(lag, level):
         stage = j - lag
         for turn in AXES:
-            orders = {part: ORDERS[(turn + part) % 3] for part in every_part}
-
-            @pl.when(jnp.logical_and(jnp.logical_and(stage >= 0, stage < TILES), stage % 3 == turn))
+            orders = {part: ORDERS[(turn + part) % THREE] for part in every_part}
+
+            @pl.when(jnp.logical_and(jnp.logical_and(stage >= 0, stage < TILES), stage % THREE == turn))
             def _(orders=orders):
                 ring.level(stage, level, orders, stage < TILES - MLP_SLOTS, stage < TILES - 1)
 
@@ -653,22 +666,29 @@
         act[at, :] = value.astype(BF)
         d = nt(dm_ref[at, :], w2) * slope
         dpre[at, :] = d.astype(BF)
-        m_acc[at, :] += nn(act[at, :], w2)
-        dh_acc[at, :] += nt(dpre[at, :], w1)
         return sum_rows(d) + total
+
+    def onward(i, carry):
+        at = pl.ds(pl.multiple_of(i * CHUNK, PACK), CHUNK)
+        m_acc[at, :] += nn(act[at, :], w2_ref[ALL].reshape(TILE, WIDTH))
+        dh_acc[at, :] += nt(dpre[at, :], w1_ref[ALL])
+        return carry
 
     def grads(core, target):
         cols = pl.ds(pl.multiple_of(core * TILE, TILE), TILE)
         g = tn(act[ALL], dm_ref[:, cols])
         for part in SIDES:
             for half in SIDES:
-                first = (part * 2 + half) * LANES
+                first = (part * PAIR + half) * LANES
                 target(part, half, g[:, first:first + LANES].reshape(CUBE + TILE_SHAPE))
 
     def grads_up(core, target):
         g = nn(turned[ALL], dpre[:, pl.ds(pl.multiple_of(core * SPAN, SPAN), SPAN)])
         for part in SIDES:
             target(part + 2, EVERY, g[:, part * LANES:part * LANES + LANES].reshape(CUBE + BLOCK))
+
+    for lag in range(ring.last + 1, 0, -1):
+        run(lag, lag - 1)
 
     @pl.when(j < TILES)
     def _():
@@ -701,9 +721,6 @@
         z_ref[0] = zo[:TOKENS]
         do_ref[ALL] = nt(da_ref[ALL], wo_ref[ALL]).astype(BF)
 
-    for lag in range(ring.last + 1, 0, -1):
-        run(lag, lag - 1)
-
     @pl.when(j < TILES)
     def _():
         slot = j % MLP_SLOTS
@@ -724,6 +741,7 @@
         ring.pair(MLP_PARTS).start()
         grads(rep, own)
         grads_up(rep, own)
+        loop(ROWS // CHUNK, onward, 0)
 
     @pl.when(j == TILES + SEQS - 1)
     def _():
@@ -781,18 +799,18 @@
 
 def attn_bwd_kernel(q_ref, k_ref, v_ref, do_ref, h_ref, wq_ref, wk_ref, wv_ref, o_ref, da_ref, x_ref, gr_ref, vec_ref,
                     gvin_ref, gbup_ref, gup_ref, gw_ref, gwo_ref, dx_ref, small_ref, up_ref,
-                    dh, grads, by_core, turned, qst, dst, xp, dxp, sums, biases, blocks, from_x, from_y, from_z, from_pair,
+                    dh, grads, by_core, turned, qst, dst, xp, gr, xs, dxs, seq_sem, dxp, sums, biases, blocks, from_x, from_y, from_z, from_pair,
                     small_send, small_recv, *ring_refs):
     g = pl.program_id(0)
 
     def window(stage, part):
         if isinstance(stage, int) and stage == 0:
-            return gwo_ref.at[:, rep * 4 + part]
-        return gw_ref.at[:, part * SUBS + (stage - 1) * 2 + rep]
+            return gwo_ref.at[:, rep * RING + part]
+        return gw_ref.at[:, part * SUBS + (stage - 1) * PAIR + rep]
 
     ring = Ring(ring_refs, ATT_SLOTS, ATT_STEPS, window)
     rep, place = ring.rep, ring.place
-    first_orders = {part: ORDERS[part % 3] for part in range(ATT_PARTS)}
+    first_orders = {part: ORDERS[part % THREE] for part in range(ATT_PARTS)}
     orders = {part: ORDERS[part] for part in range(THIRDS)}
 
     def level(stage, which, at):
@@ -855,11 +873,11 @@
         return tuple(t + n for t, n in zip(sums, out))
 
     zero = jnp.zeros((ONE, LANES), F32)
-    bias_sums = loop(SEQS, seq, (zero,) * 6, unroll=2)
+    bias_sums = loop(SEQS, seq, (zero,) * 6, unroll=3)
     for p in SIDES:
         for third in range(THIRDS):
             at = pl.multiple_of(third * WIDTH + g * GROUP + p * LANES, LANES)
-            biases[:, pl.ds(at, LANES)] = bias_sums[3 * p + third]
+            biases[:, pl.ds(at, LANES)] = bias_sums[THREE * p + third]
     poll(((2, 3), (1, 1), (0, 0)))
     stage = g + 1
 
@@ -909,19 +927,42 @@
             for stage, at in todo:
                 level(stage, orders, at)
 
+        def fetch(s):
+            rows, box = pl.ds(pl.multiple_of(s * PAD, PACK), PAD), s % PAIR
+            return (pltpu.make_async_copy(gr_ref.at[rows], gr.at[box], seq_sem.at[0, box]),
+                    pltpu.make_async_copy(x_ref.at[s], xs.at[box], seq_sem.at[1, box]))
+
+        def dx_out(s):
+            return pltpu.make_async_copy(dxs.at[s % PAIR], dx_ref.at[s], seq_sem.at[2, s % PAIR])
+
+        for copy in fetch(0):
+            copy.start()
         gain = vec_ref[:1, :]
         tail((2, 2), (3, 1), (4, 0))
         sums[ALL] = gvin_ref[ALL]
         def norm_one(s, carry):
-            padded(xp, 0, x_ref, s)
+            @pl.when(s + 1 < SEQS)
+            def _():
+                for copy in fetch(s + 1):
+                    copy.start()
+
+            for copy in fetch(s):
+                copy.wait()
+            padded(xp, 0, xs, s % PAIR)
             here = pl.ds(pl.multiple_of(s * PAD, PACK), PAD)
             centered, rstd = row_stats(xp[ALL])
             xhat = centered * rstd
             d = dh[here, :]
-            dxp[ALL] = (gr_ref[here, :] + norm_back(d * gain, xhat, rstd)).astype(BF)
+            dxp[ALL] = (gr[s % PAIR] + norm_back(d * gain, xhat, rstd)).astype(BF)
             for k, value in enumerate((d * xhat, d)):
                 sums[k:k + 1, :] += sum_rows(value)
-            dx_ref[s] = dxp[:TOKENS]
+
+            @pl.when(s >= 2)
+            def _():
+                dx_out(s - 2).wait()
+
+            dxs[s % PAIR] = dxp[:TOKENS]
+            dx_out(s).start()
 
             @pl.when(s == 3)
             def _():
@@ -930,15 +971,17 @@
             return carry
 
         loop(SEQS, norm_one, 0)
+        for s in (SEQS - 2, SEQS - 1):
+            dx_out(s).wait()
         small_blocks(blocks, sums, biases, gbup_ref)
-        at = [EVERY] * 3
+        at = [EVERY] * THREE
         number = 0
         def shard_order():
             for j in range(SUBS):
                 turned[:, j * LANES:j * LANES + LANES] = unit_columns(j)
                 for b in range(4):
                     for h in SIDES:
-                        xp[b * PACK + h * SUBS:b * PACK + h * SUBS + SUBS, j * LANES:j * LANES + LANES] = gup_ref[h, j * 4 + b]
+                        xp[b * PACK + h * SUBS:b * PACK + h * SUBS + SUBS, j * LANES:j * LANES + LANES] = gup_ref[h, j * RING + b]
             left = xp[:SHARDS]
             total = jnp.zeros_like(left)
             for _ in AXES:
@@ -970,7 +1013,7 @@
 
 def attn_bwd(qkv, do, h, w_qkv, o, da, x, gr, vec, gvin, gbup, gup):
     one = lambda shape: pl.BlockSpec(shape, lambda g: (0,) * len(shape), pipeline_mode=ONCE)
-    third = lambda t: pl.BlockSpec((ROWS, GROUP), lambda g: (0, g // 2 * 6 + t * 2 + g % 2))
+    third = lambda t: pl.BlockSpec((ROWS, GROUP), lambda g: (0, g // PAIR * 6 + t * PAIR + g % PAIR))
     wthird = lambda t: pl.BlockSpec((WIDTH, GROUP), lambda g: (0, t * GROUPS + g))
     col = pl.BlockSpec((ROWS, GROUP), lambda g: (0, g))
     anywhere = ANYWHERE
@@ -979,14 +1022,15 @@
     vmem, dma = VM, pltpu.SemaphoreType.DMA
     return pl.pallas_call(
         attn_bwd_kernel, grid=(GROUPS,),
-        out_shape=[shape((2, 3 * SUBS) + rows, F32), shape((2, SUBS) + rows, F32), shape((SEQS, TOKENS, WIDTH), BF), shape(rows, F32), shape((PACK, HIDDEN), F32)],
+        out_shape=[shape((2, THREE * SUBS) + rows, F32), shape((2, SUBS) + rows, F32), shape((SEQS, TOKENS, WIDTH), BF), shape(rows, F32), shape((PACK, HIDDEN), F32)],
         in_specs=[third(0), third(1), third(2), col, one((ROWS, WIDTH)), wthird(0), wthird(1), wthird(2),
-                  one((ROWS, WIDTH)), one((ROWS, WIDTH)), one((SEQS, TOKENS, WIDTH)), one((ROWS, WIDTH)),
+                  one((ROWS, WIDTH)), one((ROWS, WIDTH)), anywhere, anywhere,
                   one((SUBS, WIDTH)), one((SUBS, WIDTH)), one((SUBS, TILE)), one(gup.shape)],
-        out_specs=[anywhere, anywhere, one((SEQS, TOKENS, WIDTH)), one(rows), one((PACK, HIDDEN))],
-        scratch_shapes=[vmem((ROWS, WIDTH), F32), vmem((THIRDS, ROWS, GROUP), BF), vmem((ROWS, 3 * GROUP), BF),
+        out_specs=[anywhere, anywhere, anywhere, one(rows), one((PACK, HIDDEN))],
+        scratch_shapes=[vmem((ROWS, WIDTH), F32), vmem((THIRDS, ROWS, GROUP), BF), vmem((ROWS, THREE * GROUP), BF),
                         vmem((WIDTH, ROWS), BF), vmem((2, TILE, LANES), BF), vmem((2, TILE, LANES), BF),
-                        vmem((PAD, WIDTH), F32), vmem((PAD, WIDTH), BF), vmem((SUBS, WIDTH), F32), vmem((1, 3 * WIDTH), F32),
+                        vmem((PAD, WIDTH), F32), vmem((2, PAD, WIDTH), F32), vmem((2, TOKENS, WIDTH), BF), vmem((2, TOKENS, WIDTH), BF), dma((3, 2)),
+                        vmem((PAD, WIDTH), BF), vmem((SUBS, WIDTH), F32), vmem((1, THREE * WIDTH), F32),
                         vmem(CUBE + rows, F32), vmem((3, 4, 4) + rows, F32), vmem((3, 4) + rows, F32),
                         vmem((3,) + rows, F32), vmem(rows, F32), dma((10,)), dma((10,))]
         + ring_scratch(ATT_SLOTS, ATT_STAGES, ATT_PARTS),

time: 326 us -> 320 us (0.982)
  Pallas kernels: 315 us -> 308 us
where the time goes in v2:
time: 320 us; the launch traced here: 319 us
  Pallas kernels  308 us (96%)
  local copies, waits for them, and re-layouts  10.9 us (3%)
    pallas_call x1, Pallas kernels, mlp(): pl.pallas_call(mlp_kernel, grid=(TILES + SEQS,), out_shape=[shape((2, HID...  129 us
    pallas_call x1, Pallas kernels, attn_bwd(): pl.pallas_call(attn_bwd_kernel, grid=(GROUPS,), out_shape=[shape((2, THRE...  93.2 us
    pallas_call x1, Pallas kernels, first(): pl.pallas_call(first_kernel, grid=(7,), out_shape=[shape((ROWS, WIDTH), B...  86.1 us
    unnamed x19, local copies, waits for them, and re-layouts  8.18 us

profile of v2, /device:TPU:1, one launch (start us, length us, event | category | flops | bytes accessed | tf_op | source)
XLA Modules:
  0.0 319.5 jit_solution(13842274409191597133)
XLA Ops:
  0.6 86.1 %first.1 = (bf16[1248,1024]{1,0:T(8,128)(2,1)}, bf16[1248,3072]{1,0:T(8,128)(2,1)}, bf16[1248,1024]{1,0:T(8,128)(2,1)}, f32[1248,1024]{1,0:T(8,128)}, bf16[1248,...) custom-call(bf16[6,197,1024]{2,1,0:T(8,128)(2,1)} %x_ref.5, ...), custom_call_target="tpu_custom_call" | custom-call | tf_op jit(solution)/shard_map/first/pallas_call | solution.py:600
  86.7 128.6 %mlp.1 = (f32[2,32,8,128]{3,2,1,0:T(8,128)}, f32[8,8,8,128]{3,2,1,0:T(8,128)}, f32[8,512]{1,0:T(8,128)}, bf16[6,197,1024]{2,1,0:T(8,128)(2,1)}, f32[1248,1024]{1...) custom-call(bf16[1248,1024]{1,0:T(8,128)(2,1)} %get-tuple-element.34.h_ref, ...), custom_call_target="tpu_custom_call" | custom-call | tf_op jit(solution)/shard_map/mlp/pallas_call | solution.py:761
  215.4 93.2 %attn_bwd.1 = (f32[2,24,8,128]{3,2,1,0:T(8,128)}, f32[2,8,8,128]{3,2,1,0:T(8,128)}, bf16[6,197,1024]{2,1,0:T(8,128)(2,1)}, f32[8,128]{1,0:T(8,128)}, f32[16,4096]{1,0:T(8,128)}) custom-call(bf16[1248,3072]{1,0:T(8,128)(2,1)} %get-tuple-element.43.q_ref.k_ref.v_ref, bf16[1248,3072]{1,0:T(8,128)(2,1)} %get-tuple-element.43.q_ref.k_ref.v_ref, ...), custom_call_target="tpu_custom_call" | custom-call | tf_op jit(solution)/shard_map/attn_bwd/pallas_call | solution.py:1023
  308.5 0.0 copy-start
  308.5 1.4 slice_bitcast_fusion
  309.9 0.7 slice.10
  310.7 0.6 reshape.48
  311.3 3.4 %copy.25 = bf16[6,197,1024]{2,1,0:T(8,128)(2,1)} copy(bf16[6,197,1024]{2,1,0:T(8,128)(2,1)} %get-tuple-element.68) | data formatting | bytes 4841472
  314.7 0.0 copy-done
  314.7 0.0 copy-start.3
  314.7 0.0 copy-start.2
  314.7 0.0 copy-start.1
  314.7 0.0 copy-start.5
  314.7 1.4 copy.26
  316.2 0.0 copy-done.3
  316.2 0.7 copy.27
  316.8 0.0 copy-done.4
  316.8 0.6 copy.28
  317.5 0.0 copy-done.2
  317.5 0.7 copy.29
  318.2 0.0 copy-done.1
  318.2 0.7 copy.30
  318.9 0.0 copy-done.5
  318.9 0.6 copy.31
  (1 shorter events, 0.0 us)
Async XLA Ops:
  308.5 6.2 %copy-start = (bf16[6,197,1024]{2,1,0:T(8,128)(2,1)S(1)}, bf16[6,197,1024]{2,1,0:T(8,128)(2,1)}, u32[]{:S(2)}) copy-start(bf16[6,197,1024]{2,1,0:T(8,128)(2,1)} %get-tuple-element.69) | copy-start | bytes 7262212
  314.7 1.5 copy-start.3
  314.7 2.2 copy-start.4
  314.7 2.8 copy-start.2
  314.7 3.5 %copy-start.1 = (f32[8,8,8,128]{3,2,1,0:T(8,128)S(1)}, f32[8,8,8,128]{3,2,1,0:T(8,128)}, u32[]{:S(2)}) copy-start(f32[8,8,8,128]{3,2,1,0:T(8,128)} %get-tuple-element.58) | copy-start | bytes 786436
  314.7 4.2 %copy-start.5 = (f32[8,128]{1,0:T(8,128)S(1)}, f32[8,128]{1,0:T(8,128)}, u32[]{:S(2)}) copy-start(f32[8,128]{1,0:T(8,128)} %get-tuple-element.55) | copy-start | bytes 12292

commit v3 on v2

--- a/solution.py
+++ b/solution.py
@@ -1039,15 +1039,56 @@
     )(qkv, qkv, qkv, do, h, w_qkv, w_qkv, w_qkv, o, da, x, gr, vec, gvin, gbup, gup)
 
 
+def last_kernel(z_ref, dx_ref, gq_ref, go_ref, gu_ref, gd_ref, small_ref,
+                z_out, dx_out, gq_out, bq_out, go_out, gu_out, bu_out, gd_out, vec_out):
+    def untiled(src, dst):
+        for r in range(src.shape[0]):
+            for c in range(src.shape[ONE]):
+                dst[r * SUBS:r * SUBS + SUBS, c * LANES:c * LANES + LANES] = src[r, c]
+
+    z_out[ALL] = z_ref[ALL]
+    dx_out[ALL] = dx_ref[ALL]
+    untiled(gq_ref, gq_out)
+
+    @pl.when(pl.program_id(0) == 0)
+    def _():
+        untiled(go_ref, go_out)
+        untiled(gd_ref, gd_out)
+        gu_out[ALL] = gu_ref[ALL]
+        vec_out[ALL] = small_ref[:, :PACK]
+        bq_out[ALL] = pltpu.roll(small_ref[ALL], LANES - PACK, 1)[:1, 0:48]
+        lane = iota((SUBS, LANES), ONE)
+        units = jnp.zeros((ONE, LANES), F32)
+        for j in range(SUBS):
+            moved = pltpu.roll(small_ref[ALL], (SUBS * j + LANES - SHARDS) % LANES, ONE)
+            units = jnp.where(lane[:1] // SUBS == j, moved[j:j + 1], units)
+        bu_out[ALL] = units[:, :SHARDS]
+
+
+def last(z, dx, gw_qkv, gw_out, gw_up, gw_down, small):
+    whole = lambda dims: pl.BlockSpec(dims, lambda s: (0,) * len(dims), pipeline_mode=ONCE)
+    seq = pl.BlockSpec((1, TOKENS, WIDTH), lambda s: (s, 0, 0))
+    share = THREE * SUBS // SEQS
+    shape = lambda *dims: jax.ShapeDtypeStruct(dims, F32)
+    outs = [shape(PACK, THREE * WIDTH), shape(1, 48), shape(PACK, WIDTH), shape(PACK, HIDDEN), shape(1, SHARDS), shape(SHARDS, WIDTH), shape(SUBS, PACK)]
+    return pl.pallas_call(
+        last_kernel, grid=(SEQS,),
+        out_shape=[jax.ShapeDtypeStruct(z.shape, BF), jax.ShapeDtypeStruct(dx.shape, BF)] + outs,
+        in_specs=[seq, seq, pl.BlockSpec((2, share, SUBS, LANES), lambda s: (0, s, 0, 0))]
+        + [whole(g.shape) for g in (gw_out, gw_up, gw_down, small)],
+        out_specs=[seq, seq, pl.BlockSpec((PACK, share * LANES), lambda s: (0, s))] + [whole(o.shape) for o in outs[1:]],
+        name="last",
+    )(z, dx, gw_qkv, gw_out, gw_up, gw_down, small)
+
+
 def layer(x, dz, w_qkv, b_qkv, w_out, w_up, b_up, w_down, vec_params):
     h1, qkv, o, a, h2, dm, vec, b_up, w_qkv, w_out, w_up, w_down = first(
         x, dz, (w_qkv, w_out, w_up, w_down), (b_qkv[None], b_up[None], vec_params))
     w_qkv, w_out, w_up = (w.reshape(WIDTH, -1) for w in (w_qkv, w_out, w_up))
     gw_up, gw_down, gb_up, z, gr, da, do, gvec = mlp(h2, dm, w_up, b_up, w_down, x, dz, a, w_out, vec)
     gw_qkv, gw_out, dx, small, gw_up = attn_bwd(qkv, do, h1, w_qkv, o, da, x, gr, vec, gvec, gb_up, gw_up)
-    plain = lambda g: g.swapaxes(1, 2).reshape(g.shape[0] * SUBS, -1)
-    return (z, dx, plain(gw_qkv), small[0, 16:SHARDS], plain(gw_out), gw_up, small[:, 64:72].reshape(SHARDS),
-            plain(gw_down), small[:, :PACK])
+    z, dx, gw_qkv, gb_qkv, gw_out, gw_up, gb_up, gw_down, gvec = last(z, dx, gw_qkv, gw_out, gw_up, gw_down, small)
+    return z, dx, gw_qkv, gb_qkv[0], gw_out, gw_up, gb_up[0], gw_down, gvec
 
 
 def solution(mesh):

time: 320 us -> 316 us (0.988)
  local copies, waits for them, and re-layouts: 10.9 us -> 0 us
  Pallas kernels: 308 us -> 315 us
    unnamed x19 -> x0, local copies, waits for them, and re-layouts: 8.18 us -> none
    pallas_call x0 -> x1, Pallas kernels: none -> 6.59 us  [last(): pl.pallas_call(last_kernel, grid=(SEQS,), out_shape=[jax.ShapeDtypeStruct...]
where the time goes in v3:
time: 316 us; the launch traced here: 315 us
  Pallas kernels  315 us (100%)
    pallas_call x1, Pallas kernels, mlp(): pl.pallas_call(mlp_kernel, grid=(TILES + SEQS,), out_shape=[shape((2, HID...  129 us
    pallas_call x1, Pallas kernels, attn_bwd(): pl.pallas_call(attn_bwd_kernel, grid=(GROUPS,), out_shape=[shape((2, THRE...  93.2 us
    pallas_call x1, Pallas kernels, first(): pl.pallas_call(first_kernel, grid=(7,), out_shape=[shape((ROWS, WIDTH), B...  86.2 us
    pallas_call x1, Pallas kernels, last(): pl.pallas_call(last_kernel, grid=(SEQS,), out_shape=[jax.ShapeDtypeStruct...  6.59 us

profile of v3, /device:TPU:1, one launch (start us, length us, event | category | flops | bytes accessed | tf_op | source)
XLA Modules:
  0.0 315.4 jit_solution(14497403296087445471)
XLA Ops:
  0.6 86.2 %first.1 = (bf16[1248,1024]{1,0:T(8,128)(2,1)}, bf16[1248,3072]{1,0:T(8,128)(2,1)}, bf16[1248,1024]{1,0:T(8,128)(2,1)}, f32[1248,1024]{1,0:T(8,128)}, bf16[1248,...) custom-call(bf16[6,197,1024]{2,1,0:T(8,128)(2,1)} %x_ref.5, ...), custom_call_target="tpu_custom_call" | custom-call | tf_op jit(solution)/shard_map/first/pallas_call | solution.py:600
  86.8 128.6 %mlp.1 = (f32[2,32,8,128]{3,2,1,0:T(8,128)}, f32[8,8,8,128]{3,2,1,0:T(8,128)}, f32[8,512]{1,0:T(8,128)}, bf16[6,197,1024]{2,1,0:T(8,128)(2,1)}, f32[1248,1024]{1...) custom-call(bf16[1248,1024]{1,0:T(8,128)(2,1)} %get-tuple-element.43.h_ref, ...), custom_call_target="tpu_custom_call" | custom-call | tf_op jit(solution)/shard_map/mlp/pallas_call | solution.py:761
  215.4 93.2 %attn_bwd.1 = (f32[2,24,8,128]{3,2,1,0:T(8,128)}, f32[2,8,8,128]{3,2,1,0:T(8,128)}, bf16[6,197,1024]{2,1,0:T(8,128)(2,1)}, f32[8,128]{1,0:T(8,128)}, f32[16,4096]{1,0:T(8,128)}) custom-call(bf16[1248,3072]{1,0:T(8,128)(2,1)} %get-tuple-element.52.q_ref.k_ref.v_ref, bf16[1248,3072]{1,0:T(8,128)(2,1)} %get-tuple-element.52.q_ref.k_ref.v_ref, ...), custom_call_target="tpu_custom_call" | custom-call | tf_op jit(solution)/shard_map/attn_bwd/pallas_call | solution.py:1023
  308.6 6.6 %last.1 = (bf16[6,197,1024]{2,1,0:T(8,128)(2,1)}, bf16[6,197,1024]{2,1,0:T(8,128)(2,1)}, f32[16,3072]{1,0:T(8,128)}, f32[1,48]{1,0:T(1,128)}, f32[16,1024]{1,0:T...) custom-call(bf16[6,197,1024]{2,1,0:T(8,128)(2,1)} %get-tuple-element.51.z_ref, ...), custom_call_target="tpu_custom_call" | custom-call | tf_op jit(solution)/shard_map/last/pallas_call | solution.py:1074

commit v4 on v3

--- a/solution.py
+++ b/solution.py
@@ -687,7 +687,7 @@
         for part in SIDES:
             target(part + 2, EVERY, g[:, part * LANES:part * LANES + LANES].reshape(CUBE + BLOCK))
 
-    for lag in range(ring.last + 1, 0, -1):
+    for lag in range(ONE, ring.last + 2):
         run(lag, lag - 1)
 
     @pl.when(j < TILES)
@@ -1067,12 +1067,12 @@
 
 def last(z, dx, gw_qkv, gw_out, gw_up, gw_down, small):
     whole = lambda dims: pl.BlockSpec(dims, lambda s: (0,) * len(dims), pipeline_mode=ONCE)
-    seq = pl.BlockSpec((1, TOKENS, WIDTH), lambda s: (s, 0, 0))
-    share = THREE * SUBS // SEQS
+    seq = pl.BlockSpec((2, TOKENS, WIDTH), lambda s: (s, 0, 0))
+    share = SUBS
     shape = lambda *dims: jax.ShapeDtypeStruct(dims, F32)
     outs = [shape(PACK, THREE * WIDTH), shape(1, 48), shape(PACK, WIDTH), shape(PACK, HIDDEN), shape(1, SHARDS), shape(SHARDS, WIDTH), shape(SUBS, PACK)]
     return pl.pallas_call(
-        last_kernel, grid=(SEQS,),
+        last_kernel, grid=(3,),
         out_shape=[jax.ShapeDtypeStruct(z.shape, BF), jax.ShapeDtypeStruct(dx.shape, BF)] + outs,
         in_specs=[seq, seq, pl.BlockSpec((2, share, SUBS, LANES), lambda s: (0, s, 0, 0))]
         + [whole(g.shape) for g in (gw_out, gw_up, gw_down, small)],

time: 316 us -> 310 us (0.981)
  Pallas kernels: 315 us -> 309 us
    pallas_call x1, Pallas kernels: 129 us -> 123 us  [mlp(): pl.pallas_call(mlp_kernel, grid=(TILES + SEQS,), out_shape=[shape((2, HID...]
where the time goes in v4:
time: 310 us
  Pallas kernels  309 us (100%)
    pallas_call x1, Pallas kernels, mlp(): pl.pallas_call(mlp_kernel, grid=(TILES + SEQS,), out_shape=[shape((2, HID...  123 us
    pallas_call x1, Pallas kernels, attn_bwd(): pl.pallas_call(attn_bwd_kernel, grid=(GROUPS,), out_shape=[shape((2, THRE...  93.8 us
    pallas_call x1, Pallas kernels, first(): pl.pallas_call(first_kernel, grid=(7,), out_shape=[shape((ROWS, WIDTH), B...  86.2 us

profile of v4, /device:TPU:1, one launch (start us, length us, event | category | flops | bytes accessed | tf_op | source)
XLA Modules:
  0.0 310.1 jit_solution(13291159955605287359)
XLA Ops:
  0.6 86.2 %first.1 = (bf16[1248,1024]{1,0:T(8,128)(2,1)}, bf16[1248,3072]{1,0:T(8,128)(2,1)}, bf16[1248,1024]{1,0:T(8,128)(2,1)}, f32[1248,1024]{1,0:T(8,128)}, bf16[1248,...) custom-call(bf16[6,197,1024]{2,1,0:T(8,128)(2,1)} %x_ref.5, ...), custom_call_target="tpu_custom_call" | custom-call | tf_op jit(solution)/shard_map/first/pallas_call | solution.py:600
  86.8 123.3 %mlp.1 = (f32[2,32,8,128]{3,2,1,0:T(8,128)}, f32[8,8,8,128]{3,2,1,0:T(8,128)}, f32[8,512]{1,0:T(8,128)}, bf16[6,197,1024]{2,1,0:T(8,128)(2,1)}, f32[1248,1024]{1...) custom-call(bf16[1248,1024]{1,0:T(8,128)(2,1)} %get-tuple-element.43.h_ref, ...), custom_call_target="tpu_custom_call" | custom-call | tf_op jit(solution)/shard_map/mlp/pallas_call | solution.py:761
  210.1 93.8 %attn_bwd.1 = (f32[2,24,8,128]{3,2,1,0:T(8,128)}, f32[2,8,8,128]{3,2,1,0:T(8,128)}, bf16[6,197,1024]{2,1,0:T(8,128)(2,1)}, f32[8,128]{1,0:T(8,128)}, f32[16,4096]{1,0:T(8,128)}) custom-call(bf16[1248,3072]{1,0:T(8,128)(2,1)} %get-tuple-element.52.q_ref.k_ref.v_ref, bf16[1248,3072]{1,0:T(8,128)(2,1)} %get-tuple-element.52.q_ref.k_ref.v_ref, ...), custom_call_target="tpu_custom_call" | custom-call | tf_op jit(solution)/shard_map/attn_bwd/pallas_call | solution.py:1023
  303.9 6.0 %last.1 = (bf16[6,197,1024]{2,1,0:T(8,128)(2,1)}, bf16[6,197,1024]{2,1,0:T(8,128)(2,1)}, f32[16,3072]{1,0:T(8,128)}, f32[1,48]{1,0:T(1,128)}, f32[16,1024]{1,0:T...) custom-call(bf16[6,197,1024]{2,1,0:T(8,128)(2,1)} %get-tuple-element.51.z_ref, ...), custom_call_target="tpu_custom_call" | custom-call | tf_op jit(solution)/shard_map/last/pallas_call | solution.py:1074
